TPU v7x, 32 devices: a 4x4x1 block of a 4x4x8 slice. The times are simulated.
32 devices in a mesh: rep: 1 (over z), dp: 32 (over x, y, core).
Axes of the slice: x: 4, y: 4, z: 1, core: 2. Of those that a mesh axis runs over, the one named last changes fastest.
The devices are a block of a 4x4x8 slice.
Arguments:
- x: bfloat16 [32, 2048, 1152], P(('rep', 'dp'))
- dy: bfloat16 [32, 2048, 1152], P(('rep', 'dp'))
- w_gate: bfloat16 [2, 1152, 4608], replicated
- w_up: bfloat16 [2, 1152, 4608], replicated
- w_down: bfloat16 [2, 4608, 1152], replicated
- m_w_gate: float32 [2, 1152, 4608], P(None, 'dp')
- m_w_up: float32 [2, 1152, 4608], P(None, 'dp')
- m_w_down: float32 [2, 4608, 1152], P(None, 'dp')
- v_w_gate: float32 [2, 1152, 4608], P(None, 'dp')
- v_w_up: float32 [2, 1152, 4608], P(None, 'dp')
- v_w_down: float32 [2, 4608, 1152], P(None, 'dp')
Outputs:
- output 1: bfloat16 [2, 1152, 4608], P('rep')
- output 2: bfloat16 [2, 1152, 4608], P('rep')
- output 3: bfloat16 [2, 4608, 1152], P('rep')
- output 4: float32 [2, 1152, 4608], P('rep', 'dp')
- output 5: float32 [2, 1152, 4608], P('rep', 'dp')
- output 6: float32 [2, 4608, 1152], P('rep', 'dp')
- output 7: float32 [2, 1152, 4608], P('rep', 'dp')
- output 8: float32 [2, 1152, 4608], P('rep', 'dp')
- output 9: float32 [2, 4608, 1152], P('rep', 'dp')
All inputs are finite; a program needn't handle non-finite values.
Results may differ from a plain program's by a relative error of at most 0.022.
Values are sent between devices in bfloat16 or wider.
A program may use at most 768 MiB of HBM per device.

v0:
```python
import functools
import math

import jax
import jax.numpy as jnp
from jax import lax
from jax.experimental import pallas as pl
from jax.experimental.pallas import tpu as pltpu
from jax.sharding import PartitionSpec as P

F32, BF16 = jnp.float32, jnp.bfloat16
VMEM_LIMIT = 67_043_328
NN = (((1,), (0,)), ((), ()))
NT = (((1,), (1,)), ((), ()))
TN = (((0,), (0,)), ((), ()))


def dot(a, b, dims=NN):
    return lax.dot_general(a, b, dims, preferred_element_type=F32)


def sigmoid(x):
    return 1.0 / (1.0 + jnp.exp(-x))


def whole(shape):
    return pl.BlockSpec(shape, lambda *_: (0,) * len(shape), pipeline_mode=pl.Buffered(1))


def call(body, flops, moved, params=None, **kw):
    return pl.pallas_call(
        body,
        cost_estimate=pl.CostEstimate(flops=int(flops), bytes_accessed=int(moved), transcendentals=0),
        compiler_params=pltpu.CompilerParams(**{"vmem_limit_bytes": VMEM_LIMIT, **(params or {})}),
        **kw,
    )


def row_scale(wide):
    return lax.rsqrt(jnp.mean(wide * wide, -1, keepdims=True) + 1e-6)


def hidden_forward(layer, x, w_gate, w_up):
    tokens, d = x.shape
    ff = w_gate.shape[-1]
    bf, bm = 256, 512
    n = tokens // bm

    def body(x, wg, wu, gate, up, hid, a_t, x_in, a, came):
        j = pl.program_id(0)

        def rows(i):
            return pl.ds(pl.multiple_of(i * bm, bm), bm)

        def come(i):
            return pltpu.make_async_copy(x.at[rows(i)], x_in.at[rows(i)], came.at[i])

        def chunk(r):
            g, u = dot(a[r, :], wg[...]), dot(a[r, :], wu[...])
            gate[r, :] = g
            up[r, :] = u
            hid[r, :] = (g * sigmoid(g) * u).astype(BF16)

        @pl.when(j == 0)
        def _():
            for i in range(n):
                come(i).start()

            def first(i, _):
                come(i).wait()
                wide = x_in[rows(i), :].astype(F32)
                a[rows(i), :] = (wide * row_scale(wide)).astype(BF16)
                chunk(rows(i))
                return 0

            lax.fori_loop(0, n, first, 0)

        @pl.when(j > 0)
        def _():
            for i in range(n):
                chunk(slice(i * bm, (i + 1) * bm))

        @pl.when(j == 1)
        def _():
            a_t[...] = a[...].T

    w_spec = pl.BlockSpec((None, d, bf), lambda j: (layer, 0, j))
    o_spec = pl.BlockSpec((tokens, bf), lambda j: (0, j))
    wide = jax.ShapeDtypeStruct((tokens, ff), F32)
    return call(
        body,
        4 * tokens * d * ff,
        10 * tokens * ff + 4 * d * ff,
        name="hidden_forward",
        grid=(ff // bf,),
        in_specs=[pl.BlockSpec(memory_space=pl.ANY), w_spec, w_spec],
        out_specs=[*[o_spec] * 3, whole((d, tokens))],
        out_shape=(wide, wide, jax.ShapeDtypeStruct((tokens, ff), BF16), jax.ShapeDtypeStruct((d, tokens), BF16)),
        scratch_shapes=[pltpu.VMEM((tokens, d), BF16), pltpu.VMEM((tokens, d), BF16), pltpu.SemaphoreType.DMA((n,))],
    )(x, w_gate, w_up)


def down_forward(layer, x, hid, w_down):
    tokens, ff = hid.shape
    d = x.shape[-1]
    bm = 256

    def body(x, hid, wd, h1, a1, a1_t):
        h = (x[...].astype(F32) + dot(hid[...], wd[...]).astype(BF16).astype(F32)).astype(BF16)
        h1[...] = h
        wide = h.astype(F32)
        unit = wide * row_scale(wide)
        a1[...] = unit.astype(BF16)
        a1_t[...] = unit.T.astype(BF16)

    rows = pl.BlockSpec((bm, d), lambda i: (i, 0))
    out = jax.ShapeDtypeStruct((tokens, d), BF16)
    return call(
        body,
        2 * tokens * d * ff,
        2 * tokens * ff + 2 * d * ff,
        name="down_forward",
        grid=(tokens // bm,),
        in_specs=[
            rows,
            pl.BlockSpec((bm, ff), lambda i: (i, 0)),
            pl.BlockSpec((None, ff, d), lambda i: (layer, 0, 0), pipeline_mode=pl.Buffered(1)),
        ],
        out_specs=[rows, rows, pl.BlockSpec((d, bm), lambda i: (0, i))],
        out_shape=(out, out, jax.ShapeDtypeStruct((d, tokens), BF16)),
    )(x, hid, w_down)


def gate_up_cotangents(g, u, dh):
    dh = dh.astype(BF16).astype(F32)
    s = sigmoid(g)
    silu = g * s
    return (dh * u * (s + silu * (1.0 - s))).astype(BF16), (dh * silu).astype(BF16), (silu * u).astype(BF16)


def last_layer(layer, a, dy, w_gate, w_up, w_down):
    tokens, d = a.shape
    ff = w_gate.shape[-1]
    bf, bm = 256, 512

    def body(a, dy, wg, wu, wd, hid, dg, du):
        for i in range(tokens // bm):
            r = slice(i * bm, (i + 1) * bm)
            g, u = dot(a[r, :], wg[...]), dot(a[r, :], wu[...])
            dg[r, :], du[r, :], hid[r, :] = gate_up_cotangents(g, u, dot(dy[r, :], wd[...], NT))

    w_spec = pl.BlockSpec((None, d, bf), lambda j: (layer, 0, j))
    o_spec = pl.BlockSpec((tokens, bf), lambda j: (0, j))
    out = jax.ShapeDtypeStruct((tokens, ff), BF16)
    return call(
        body,
        6 * tokens * d * ff,
        6 * tokens * ff + 6 * d * ff,
        name="last_layer",
        grid=(ff // bf,),
        in_specs=[whole((tokens, d)), whole((tokens, d)), w_spec, w_spec, pl.BlockSpec((None, bf, d), lambda j: (layer, j, 0))],
        out_specs=[o_spec] * 3,
        out_shape=(out, out, out),
    )(a, dy, w_gate, w_up, w_down)


def states_cotangent(layer, h, dy, dg, du, w_gate, w_up):
    tokens, ff = dg.shape
    d = h.shape[-1]
    bm, bk = 256, 512
    n = ff // bk

    def body(h, dy, dg, du, wg, wu, out, w, total, came):
        def k(c):
            return pl.ds(pl.multiple_of(c * bk, bk), bk)

        def come(c):
            return [pltpu.make_async_copy(t.at[layer, :, k(c)], w.at[i, :, k(c)], came.at[i, c]) for i, t in enumerate((wg, wu))]

        def rest(da):
            wide = h[...].astype(F32)
            da = da.astype(BF16).astype(F32)
            s = row_scale(wide)
            back = da * s - wide * (s * s * s * jnp.mean(da * wide, -1, keepdims=True))
            out[...] = (dy[...].astype(F32) + back).astype(BF16)

        @pl.when(pl.program_id(0) == 0)
        def _():
            for c in range(n):
                for copy in come(c):
                    copy.start()
            total[...] = jnp.zeros_like(total)

            def add(c, _):
                for copy in come(c):
                    copy.wait()
                total[...] += dot(dg[:, k(c)], w[0, :, k(c)], NT) + dot(du[:, k(c)], w[1, :, k(c)], NT)
                return 0

            lax.fori_loop(0, n, add, 0)
            rest(total[...])

        @pl.when(pl.program_id(0) > 0)
        def _():
            rest(dot(dg[...], w[0], NT) + dot(du[...], w[1], NT))

    rows = pl.BlockSpec((bm, d), lambda i: (i, 0))
    wide_rows = pl.BlockSpec((bm, ff), lambda i: (i, 0))
    anywhere = pl.BlockSpec(memory_space=pl.ANY)
    return call(
        body,
        4 * tokens * d * ff,
        4 * tokens * ff + 4 * d * ff,
        name="states_cotangent",
        grid=(tokens // bm,),
        in_specs=[rows, rows, wide_rows, wide_rows, anywhere, anywhere],
        out_specs=rows,
        out_shape=jax.ShapeDtypeStruct((tokens, d), BF16),
        scratch_shapes=[pltpu.VMEM((2, d, ff), BF16), pltpu.VMEM((bm, d), F32), pltpu.SemaphoreType.DMA((2, n))],
    )(h, dy, dg, du, w_gate, w_up)


SLOTS, ARRIVALS = 3, 4


def pair_scratch(rows, columns):
    return [
        pltpu.VMEM((SLOTS, 2, rows, columns), BF16),
        pltpu.VMEM((ARRIVALS, rows, columns), BF16),
        pltpu.SemaphoreType.DMA((SLOTS,)),
        pltpu.SemaphoreType.DMA((ARRIVALS,)),
    ]


def pair_step(n, make, out, made, came, sent, arrived):
    j = pl.program_id(0)
    me = lax.axis_index("dp")
    core = lax.rem(me, 2)
    other = me + 1 - 2 * core

    def transfer(step):
        slot, place = lax.rem(step, SLOTS), lax.rem(step, ARRIVALS)
        return pltpu.make_async_remote_copy(
            src_ref=made.at[slot, 1 - core],
            dst_ref=came.at[place],
            send_sem=sent.at[slot],
            recv_sem=arrived.at[place],
            device_id={"dp": other},
            device_id_type=pl.DeviceIdType.MESH,
        )

    @pl.when(j == 0)
    def _():
        barrier = pltpu.get_barrier_semaphore()
        pl.semaphore_signal(barrier, inc=1, device_id={"dp": other}, device_id_type=pl.DeviceIdType.MESH)
        pl.semaphore_wait(barrier, 1)

    @pl.when(j >= 2)
    def _():
        transfer(j - 2).wait()
        own = made[lax.rem(j - 2, SLOTS), core]
        out[...] = (own.astype(F32) + came[lax.rem(j - 2, ARRIVALS)].astype(F32)).astype(BF16)

    @pl.when(j < n)
    def _():
        make(made.at[lax.rem(j, SLOTS)])
        transfer(j).start()


def pair_params(number):
    return {"collective_id": number, "has_side_effects": True}


def down_gradient(number, hid, dy):
    tokens, ff = hid.shape
    d = dy.shape[-1]
    chips = lax.axis_size("dp") // 2
    own = ff // (2 * chips)
    bf = 1152
    n, per = ff // bf, bf // (2 * own)

    def body(hid, dy, out, *scratch):
        def make(slot):
            block = dot(hid[...], dy[...], TN)
            for i in range(per):
                for half in range(2):
                    at = (2 * i + half) * own
                    slot[half, i * own : (i + 1) * own, :] = block[at : at + own].astype(BF16)

        pair_step(n, make, out, *scratch)

    return call(
        body,
        2 * tokens * d * ff,
        2 * tokens * ff + d * ff,
        pair_params(number),
        name=f"down_gradient_{number}",
        grid=(n + 2,),
        in_specs=[pl.BlockSpec((tokens, bf), lambda j: (0, jnp.minimum(j, n - 1))), whole((tokens, d))],
        out_specs=pl.BlockSpec((bf // 2, d), lambda j: (jnp.maximum(j - 2, 0), 0)),
        out_shape=jax.ShapeDtypeStruct((ff // 2, d), BF16),
        scratch_shapes=pair_scratch(bf // 2, d),
    )(hid, dy)


PART = 256


def halves_specs(shape, first, n, half, layer=None, transposed=False):
    def spec(h):
        def at(j):
            k = h * half + first + jnp.minimum(j, n - 1)
            index = (k, 0) if transposed else (0, k)
            return index if layer is None else (layer, *index)

        return pl.BlockSpec(shape, at)

    return [spec(0), spec(1)]


def gate_up_gradient(number, first, n, a_t, dg, du):
    d, tokens = a_t.shape
    half = dg.shape[-1] // (2 * PART)

    def body(a_t, dg0, dg1, du0, du1, out, *scratch):
        def make(slot):
            for h, (dg, du) in enumerate(((dg0, du0), (dg1, du1))):
                slot[h, :, :PART] = dot(a_t[...], dg[...]).astype(BF16)
                slot[h, :, PART:] = dot(a_t[...], du[...]).astype(BF16)

        pair_step(n, make, out, *scratch)

    t_specs = halves_specs((tokens, PART), first, n, half)
    return call(
        body,
        8 * tokens * d * PART * n,
        8 * tokens * PART * n,
        pair_params(number),
        name=f"gate_up_gradient_{number}",
        grid=(n + 2,),
        in_specs=[whole((d, tokens)), *t_specs, *t_specs],
        out_specs=pl.BlockSpec((d, 2 * PART), lambda j: (0, jnp.maximum(j - 2, 0))),
        out_shape=jax.ShapeDtypeStruct((d, 2 * PART * n), BF16),
        scratch_shapes=pair_scratch(d, 2 * PART),
    )(a_t, dg, dg, du, du)


SIDE = 4
PLACES = 4


def first_layer_gradient(number, layer, a_t, dy, gate, up, w_down):
    d, tokens = a_t.shape
    half = gate.shape[-1] // (2 * PART)
    n = half
    bm = 512
    rows = d // SIDE**2
    mid = PART // 2

    def body(a_t, dy, g0, g1, u0, u1, w0, w1, out, dg, du, made, came, sums, across1, pass1, got1, total1, across2, pass2, got2, ps, pr, sent, arrived):
        j = pl.program_id(0)
        me = lax.axis_index("dp")
        core = lax.rem(me, 2)
        other = me + 1 - 2 * core
        x, y = lax.div(me, 2 * SIDE), lax.rem(lax.div(me, 2), SIDE)

        def at(x, y):
            return {"dp": (x * SIDE + y) * 2 + core}

        def beside(axis, way):
            to = lax.rem((x if axis == 0 else y) + (1 if way == 0 else SIDE - 1), SIDE)
            return at(to, y) if axis == 0 else at(x, to)

        here = (x, y)

        def transfer(stage, color, way, block):
            place, slot = lax.rem(block, PLACES), lax.rem(block, SLOTS)
            first, second = color, 1 - color
            columns = slice(color * PART, (color + 1) * PART)
            if stage == 1:
                far = lax.rem(here[first] + 2, SIDE)
                part = slice(2 * way, 2 * way + 2)
                src = sums.at[slot, far, part, :, columns] if color == 0 else sums.at[slot, part, far, :, columns]
                dst = across1.at[color, place, way]
            elif stage == 2:
                src, dst = pass1.at[color, place, way], got1.at[color, place, way]
            elif stage == 3:
                far = lax.rem(here[second] + 2, SIDE)
                src = total1.at[color, place, far, :, slice(way * mid, (way + 1) * mid)]
                dst = across2.at[color, place, way]
            else:
                src, dst = pass2.at[color, place, way], got2.at[color, place, way]
            index = ((stage - 1) * 2 + color) * 2 + way
            return pltpu.make_async_remote_copy(
                src_ref=src,
                dst_ref=dst,
                send_sem=sent.at[index, place],
                recv_sem=arrived.at[index, place],
                device_id=beside(first if stage <= 2 else second, way),
                device_id_type=pl.DeviceIdType.MESH,
            )

        def swap(block):
            slot, place = lax.rem(block, SLOTS), lax.rem(block, PLACES)
            return pltpu.make_async_remote_copy(
                src_ref=made.at[slot, 1 - core],
                dst_ref=came.at[place],
                send_sem=ps.at[slot],
                recv_sem=pr.at[place],
                device_id={"dp": other},
                device_id_type=pl.DeviceIdType.MESH,
            )

        def of(color, slot, i):
            columns = slice(color * PART, (color + 1) * PART)
            t = sums[slot, i, :, :, columns] if color == 0 else sums[slot, :, i, :, columns]
            return t.astype(F32)

        def stage(lag, act):
            @pl.when((j >= lag) & (j < n + lag))
            def _():
                act(j - lag)

        @pl.when(j == 0)
        def _():
            barrier = pltpu.get_barrier_semaphore()
            for peer in ({"dp": other}, beside(0, 0), beside(0, 1), beside(1, 0), beside(1, 1)):
                pl.semaphore_signal(barrier, inc=1, device_id=peer, device_id_type=pl.DeviceIdType.MESH)
            pl.semaphore_wait(barrier, 5)

        def last(block):
            place = lax.rem(block, PLACES)
            for color in range(2):
                for way in range(2):
                    transfer(4, color, way, block).wait()
                b = here[1 - color]
                t = total1[color, place, b].astype(F32) + got2[color, place, 0].astype(F32) + got2[color, place, 1].astype(F32)
                out[color] = t.astype(BF16)

        def fourth(block):
            place = lax.rem(block, PLACES)
            for color in range(2):
                for way in range(2):
                    transfer(3, color, way, block).wait()
                for way in range(2):
                    b = lax.rem(here[1 - color] + (1 if way == 0 else SIDE - 1), SIDE)
                    pass2[color, place, way] = total1[color, place, b]
                    c = slice(way * mid, (way + 1) * mid)
                    more = total1[color, place, b, :, c].astype(F32) + across2[color, place, way].astype(F32)
                    pass2[color, place, way, :, c] = more.astype(BF16)
                    transfer(4, color, way, block).start()

        def third(block):
            place, slot = lax.rem(block, PLACES), lax.rem(block, SLOTS)
            for color in range(2):
                for way in range(2):
                    transfer(2, color, way, block).wait()
                t = of(color, slot, here[color]) + got1[color, place, 0].astype(F32) + got1[color, place, 1].astype(F32)
                total1[color, place] = t.astype(BF16)
                for way in range(2):
                    transfer(3, color, way, block).start()

        def second(block):
            place, slot = lax.rem(block, PLACES), lax.rem(block, SLOTS)
            for color in range(2):
                for way in range(2):
                    transfer(1, color, way, block).wait()
                for way in range(2):
                    t = of(color, slot, lax.rem(here[color] + (1 if way == 0 else SIDE - 1), SIDE))
                    p = slice(2 * way, 2 * way + 2)
                    q = slice(2 - 2 * way, 4 - 2 * way)
                    pass1[color, place, way, p] = (t[p] + across1[color, place, way].astype(F32)).astype(BF16)
                    pass1[color, place, way, q] = t[q].astype(BF16)
                    transfer(2, color, way, block).start()

        def first(block):
            place, slot = lax.rem(block, PLACES), lax.rem(block, SLOTS)
            swap(block).wait()
            for k in range(SIDE**2):
                r = slice(k * rows, (k + 1) * rows)
                t = made[slot, core, r, :].astype(F32) + came[place, r, :].astype(F32)
                sums[slot, k // SIDE, k % SIDE] = t.astype(BF16)
            for color in range(2):
                for way in range(2):
                    transfer(1, color, way, block).start()

        def make(block):
            slot = lax.rem(block, SLOTS)
            for h, (g, u, w) in enumerate(((g0, u0, w0), (g1, u1, w1))):
                for i in range(tokens // bm):
                    r = slice(i * bm, (i + 1) * bm)
                    dg[h, r, :], du[h, r, :], _ = gate_up_cotangents(g[r, :], u[r, :], dot(dy[r, :], w[...], NT))
                made[slot, h, :, :PART] = dot(a_t[...], dg[h]).astype(BF16)
                made[slot, h, :, PART:] = dot(a_t[...], du[h]).astype(BF16)
            swap(block).start()

        stage(6, last)
        stage(5, fourth)
        stage(4, third)
        stage(3, second)
        stage(2, first)
        stage(0, make)

    t_specs = halves_specs((tokens, PART), 0, n, half)
    block = (SIDE, rows, PART)
    return call(
        body,
        12 * tokens * d * PART * n,
        16 * tokens * PART * n,
        pair_params(number),
        name="first_layer_gradient",
        grid=(n + 6,),
        in_specs=[whole((d, tokens)), whole((tokens, d)), *t_specs, *t_specs, *halves_specs((None, PART, d), 0, n, half, layer, True)],
        out_specs=pl.BlockSpec((2, rows, PART), lambda j: (0, 0, jnp.maximum(j - 6, 0))),
        out_shape=jax.ShapeDtypeStruct((2, rows, PART * n), BF16),
        scratch_shapes=[
            pltpu.VMEM((2, tokens, PART), BF16),
            pltpu.VMEM((2, tokens, PART), BF16),
            pltpu.VMEM((SLOTS, 2, d, 2 * PART), BF16),
            pltpu.VMEM((PLACES, d, 2 * PART), BF16),
            pltpu.VMEM((SLOTS, SIDE, SIDE, rows, 2 * PART), BF16),
            pltpu.VMEM((2, PLACES, 2, SIDE // 2, rows, PART), BF16),
            pltpu.VMEM((2, PLACES, 2, *block), BF16),
            pltpu.VMEM((2, PLACES, 2, *block), BF16),
            pltpu.VMEM((2, PLACES, *block), BF16),
            pltpu.VMEM((2, PLACES, 2, rows, mid), BF16),
            pltpu.VMEM((2, PLACES, 2, rows, PART), BF16),
            pltpu.VMEM((2, PLACES, 2, rows, PART), BF16),
            pltpu.SemaphoreType.DMA((SLOTS,)),
            pltpu.SemaphoreType.DMA((PLACES,)),
            pltpu.SemaphoreType.DMA((16, PLACES)),
            pltpu.SemaphoreType.DMA((16, PLACES)),
        ],
    )(a_t, dy, gate, gate, up, up, w_down, w_down)


def updated_and_gathered(number, gate_up0, gate_up1, down0, down1, w_gate, w_up, w_down, m_gate, m_up, m_down, v_gate, v_up, v_down):
    n = lax.axis_size("dp")
    layers, d, ff = w_gate.shape
    rows, half = gate_up0.shape[1:]
    own_rows, moment_rows = ff // n, d // n
    steps = half // PART
    width = 2 * half + d
    cut = -(-width // 256) * 128
    count = 3 * layers * d * ff
    parts = (slice(0, cut), slice(cut, width))
    plan = []

    def body(gu0, gu1, d0, d1, wg, wu, wd, mg, mu, md, vg, vu, vd, ag, wd1, nmg, nmu, nmd, nvg, nvu, nvd,
             w_gu, w_d, mom, mom_d, packs, spare, tile, tiles, load, swap_s, swap_r, norm_s, norm_r, sent, arrived):
        me = lax.axis_index("dp")
        core = lax.rem(me, 2)
        other = me + 1 - 2 * core
        chip = lax.div(me, 2)
        x, y = lax.div(chip, SIDE), lax.rem(chip, SIDE)
        here = (x, y)
        mine, theirs = (pl.ds(pl.multiple_of(c * half, 128), half) for c in (core, 1 - core))

        moments = (mg, mu, vg, vu)
        new_moments = (nmg, nmu, nvg, nvu)
        loads = [
            *[(t.at[:, :, mine], mom.at[k, core]) for k, t in enumerate(moments)],
            (md, mom_d.at[0]),
            (vd, mom_d.at[1]),
            (wg.at[:, pl.ds(pl.multiple_of(chip * rows, 8), rows), mine], w_gu.at[0]),
            (wu.at[:, pl.ds(pl.multiple_of(chip * rows, 8), rows), mine], w_gu.at[1]),
            (wd.at[:, pl.ds(pl.multiple_of(me * own_rows, 16), own_rows), :], w_d),
        ]
        loads = [pltpu.make_async_copy(a, b, load.at[k]) for k, (a, b) in enumerate(loads)]
        for copy in loads:
            copy.start()

        barrier = pltpu.get_barrier_semaphore()

        def greet(i, _):
            pl.semaphore_signal(barrier, inc=1, device_id={"dp": lax.rem(me + i, n)}, device_id_type=pl.DeviceIdType.MESH)
            return 0

        lax.fori_loop(1, n, greet, 0)

        def square(t):
            t = t.astype(F32)
            t = t * t
            return sum(t[k * 8 : (k + 1) * 8] for k in range(t.shape[0] // 8))

        def squares(k, total):
            at = pl.ds(pl.multiple_of(k * PART, PART), PART)
            both = pl.ds(pl.multiple_of(k * 2 * PART, PART), 2 * PART)
            two = square(gu1[:, both])
            return total + square(gu0[0, :, at]) + square(gu0[1, :, at]) + two[:, :PART] + two[:, PART:]

        total = lax.fori_loop(0, steps, squares, jnp.zeros((8, PART), F32))
        downs = square(d0[...]) + square(d1[...])
        total = total[:, :128] + total[:, 128:] + sum(downs[:, k * 128 : (k + 1) * 128] for k in range(d // 128))
        tile[...] = total
        tiles[0] = total

        pl.semaphore_wait(barrier, n - 1)

        def swap(src, dst, k):
            return pltpu.make_async_remote_copy(
                src_ref=src, dst_ref=dst, send_sem=swap_s.at[k], recv_sem=swap_r.at[k], device_id={"dp": other}, device_id_type=pl.DeviceIdType.MESH
            )

        def size(i):
            return pltpu.make_async_remote_copy(
                src_ref=tile,
                dst_ref=tiles.at[i],
                send_sem=norm_s.at[i],
                recv_sem=norm_r.at[i],
                device_id={"dp": lax.rem(me + i, n)},
                device_id_type=pl.DeviceIdType.MESH,
            )

        lax.fori_loop(1, n, lambda i, _: (size(i).start(), 0)[1], 0)
        swaps = [swap(t.at[:, :, theirs], mom.at[k, core], k) for k, t in enumerate(moments)]
        for copy in swaps:
            copy.start()
        for copy in loads:
            copy.wait()
        for copy in swaps:
            copy.wait()
        lax.fori_loop(1, n, lambda i, _: (size(i).wait(), 0)[1], 0)
        total = lax.fori_loop(0, n, lambda i, total: total + tiles[lax.rem(me - i + n, n)], jnp.zeros((8, 128), F32))
        total = jnp.sum(jnp.sum(total, 0, keepdims=True), 1, keepdims=True)
        factor = jnp.minimum(1.0, 0.5 * lax.rsqrt(total / count + 1e-30))

        def adamw(w, m, v, g):
            g = g * factor
            m = 0.9 * m + 0.1 * g
            v = 0.95 * v + 0.05 * g * g
            return w - 0.02 * (m * lax.rsqrt(v + 1e-8) + 0.1 * w), m, v

        def step_gate_up(layer):
            for gu in range(2):

                def columns(k, _, gu=gu):
                    at = pl.ds(pl.multiple_of(k * PART, PART), PART)
                    if layer == 0:
                        g = gu0[gu, :, at]
                    else:
                        g = gu1[:, pl.ds(pl.multiple_of((2 * k + gu) * PART, PART), PART)]
                    g = g.astype(F32)
                    w = w_gu[gu, layer, :, at].astype(F32)
                    new = []
                    for r in range(2):
                        p = slice(r * moment_rows, (r + 1) * moment_rows)
                        one, m, v = adamw(w[p], mom[gu, r, layer, :, at], mom[2 + gu, r, layer, :, at], g[p])
                        mom[gu, r, layer, :, at] = m
                        mom[2 + gu, r, layer, :, at] = v
                        new.append(one)
                    packs[layer, :, pl.ds(pl.multiple_of(gu * half + k * PART, PART), PART)] = jnp.concatenate(new, 0).astype(BF16)
                    return 0

                lax.fori_loop(0, steps, columns, 0)

        def step_down(layer, p, g):
            new, m, v = adamw(w_d[layer, p, :].astype(F32), mom_d[0, layer, p, :], mom_d[1, layer, p, :], g[p, :].astype(F32))
            mom_d[0, layer, p, :] = m
            mom_d[1, layer, p, :] = v
            return new.astype(BF16)

        def place(color, i, k, whose, part):
            i, k = (lax.rem(t + SIDE, SIDE) for t in (i, k))
            a, b = (i, k) if color == 0 else (k, i)
            return ag.at[a, b, whose, color, :, parts[part]]

        def beside(axis, way):
            to = lax.rem(here[axis] + (1 if way == 0 else SIDE - 1), SIDE)
            a, b = (to, y) if axis == 0 else (x, to)
            return {"dp": (a * SIDE + b) * 2 + core}

        started = {}

        def send(name, color, o, q, part, to):
            index = len(plan) if name not in plan else plan.index(name)
            if name not in plan:
                plan.append(name)
            dst = place(color, here[color] + o, here[1 - color] + q, core, part)
            src = packs.at[color, :, parts[part]] if (o, q) == (0, 0) else dst
            copy = pltpu.make_async_remote_copy(
                src_ref=src, dst_ref=dst, send_sem=sent.at[index], recv_sem=arrived.at[index], device_id=to, device_id_type=pl.DeviceIdType.MESH
            )
            copy.start()
            started[name] = copy

        def along_first(color, way, part):
            send(("a", color, way, part), color, 0, 0, part, beside(color, way))

        def on_first(color, way):
            send(("b", color, way), color, -1 if way == 0 else 1, 0, way, beside(color, way))

        def along_second(color, o, part):
            for way in range(2):
                send(("c", color, way, o, part), color, o, 0, part, beside(1 - color, way))

        def on_second(color, way, o):
            send(("d", color, way, o), color, o, -1 if way == 0 else 1, way, beside(1 - color, way))

        def share(color, o, q, part):
            send(("e", color, o, q, part), color, o, q, part, {"dp": other})

        def own(color):
            for part in range(2):
                for way in range(2):
                    along_first(color, way, part)
            for part in range(2):
                along_second(color, 0, part)
                share(color, 0, 0, part)
            copy = pltpu.make_async_copy(packs.at[color], ag.at[x, y, core, color], load.at[color])
            copy.start()
            return copy

        step_gate_up(0)
        packs[0, :, 2 * half :] = step_down(0, slice(0, rows), d0)
        kept = [own(0)]
        step_gate_up(1)
        packs[1, :, 2 * half :] = step_down(0, slice(rows, 2 * rows), d0)
        kept.append(own(1))
        spare[...] = step_down(1, slice(0, own_rows), d1)

        stores = [
            *[(mom.at[k, core], t.at[:, :, mine]) for k, t in enumerate(new_moments)],
            (mom_d.at[0], nmd),
            (mom_d.at[1], nvd),
            (spare, wd1),
        ]
        stores = [pltpu.make_async_copy(a, b, load.at[2 + k]) for k, (a, b) in enumerate(stores)]
        backs = [swap(mom.at[k, 1 - core], t.at[:, :, mine], 4 + k) for k, t in enumerate(new_moments)]
        for copy in (*stores, *backs):
            copy.start()

        both = [(color, way) for color in range(2) for way in range(2)]
        for part in range(2):
            for color, way in both:
                started["a", color, way, part].wait_recv()
                if way == part:
                    on_first(color, way)
                o = -1 if way == 0 else 1
                along_second(color, o, part)
                share(color, o, 0, part)

        def arrivals(o):
            for part in range(2):
                for color, way in both:
                    started["c", color, way, o, part].wait_recv()
                    if way == part:
                        on_second(color, way, o)
                    share(color, o, -1 if way == 0 else 1, part)

        arrivals(0)
        for color, way in both:
            started["b", color, way].wait_recv()
            along_second(color, 2, way)
            share(color, 2, 0, way)
        for o in (-1, 1, 2):
            arrivals(o)
        for o in (0, -1, 1, 2):
            for color, way in both:
                started["d", color, way, o].wait_recv()
                share(color, o, 2, way)
        for name, copy in started.items():
            copy.wait_send()
            if name[0] == "e":
                copy.wait_recv()
        for copy in (*kept, *stores, *backs):
            copy.wait()

    anywhere = pl.BlockSpec(memory_space=pl.ANY)
    vmem = pl.BlockSpec(memory_space=pltpu.VMEM)
    return call(
        body,
        1e9,
        1e8,
        pair_params(number),
        name="updated_and_gathered",
        in_specs=[vmem] * 4 + [anywhere] * 9,
        out_specs=[anywhere] * 8,
        out_shape=[
            jax.ShapeDtypeStruct((SIDE, SIDE, 2, 2, rows, width), BF16),
            jax.ShapeDtypeStruct((own_rows, d), BF16),
            *[jax.ShapeDtypeStruct(t.shape, F32) for t in (m_gate, m_up, m_down, v_gate, v_up, v_down)],
        ],
        scratch_shapes=[
            pltpu.VMEM((2, layers, rows, half), BF16),
            pltpu.VMEM((layers, own_rows, d), BF16),
            pltpu.VMEM((4, 2, layers, moment_rows, half), F32),
            pltpu.VMEM((2, layers, own_rows, d), F32),
            pltpu.VMEM((2, rows, width), BF16),
            pltpu.VMEM((own_rows, d), BF16),
            pltpu.VMEM((8, 128), F32),
            pltpu.VMEM((n, 8, 128), F32),
            pltpu.SemaphoreType.DMA((9,)),
            pltpu.SemaphoreType.DMA((8,)),
            pltpu.SemaphoreType.DMA((8,)),
            pltpu.SemaphoreType.DMA((n,)),
            pltpu.SemaphoreType.DMA((n,)),
            pltpu.SemaphoreType.DMA((124,)),
            pltpu.SemaphoreType.DMA((124,)),
        ],
    )(gate_up0, gate_up1, down0, down1, w_gate, w_up, w_down, m_gate, m_up, m_down, v_gate, v_up, v_down)


def placed(packs, layers, d, ff):
    rows, width = packs.shape[-2:]
    half = ff // 2
    per = 2

    def body(t, gate, up, down):
        for b in range(per):
            for core in range(2):
                for color in range(2):
                    r = slice(b * rows, (b + 1) * rows)
                    c = slice(core * half, (core + 1) * half)
                    gate[color, r, c] = t[b, core, color, :, :half]
                    up[color, r, c] = t[b, core, color, :, half : 2 * half]
                    at = ((b * 2 + core) * 2 + color) * rows
                    down[at : at + rows, :] = t[b, core, color, :, 2 * half :]

    n = SIDE // per
    out = pl.BlockSpec((layers, per * rows, ff), lambda i, j: (0, i * n + j, 0))
    return call(
        body,
        1,
        4 * packs.size,
        name="placed",
        grid=(SIDE, n),
        in_specs=[pl.BlockSpec((None, per, 2, 2, rows, width), lambda i, j: (i, j, 0, 0, 0, 0))],
        out_specs=[out, out, pl.BlockSpec((None, per * 4 * rows, d), lambda i, j: (0, i * n + j, 0))],
        out_shape=[jax.ShapeDtypeStruct((layers, d, ff), BF16)] * 2 + [jax.ShapeDtypeStruct((layers, ff, d), BF16)],
    )(packs)


def copied(*arrays):
    def body(*refs):
        for a, b in zip(refs[: len(arrays)], refs[len(arrays) :], strict=True):
            b[...] = a[...]

    specs = [pl.BlockSpec((1, *t.shape[1:]), lambda i: (i, 0, 0)) for t in arrays]
    return call(
        body,
        1,
        sum(8 * t.size for t in arrays),
        name="copied",
        grid=(arrays[0].shape[0],),
        in_specs=specs,
        out_specs=specs,
        out_shape=[jax.ShapeDtypeStruct(t.shape, t.dtype) for t in arrays],
    )(*arrays)


def placed_last(down, gathered):
    layers, ff, d = down.shape
    bm = 1152

    def body(down, t, out):
        out[...] = t[...]

    return call(
        body,
        1,
        4 * gathered.size,
        name="placed_last",
        grid=(ff // bm,),
        in_specs=[pl.BlockSpec(memory_space=pl.ANY), pl.BlockSpec((bm, d), lambda i: (i, 0))],
        out_specs=pl.BlockSpec((None, bm, d), lambda i: (layers - 1, i, 0)),
        out_shape=jax.ShapeDtypeStruct(down.shape, BF16),
        input_output_aliases={0: 0},
    )(down, gathered)


def solution(mesh):
    chips = mesh.shape["dp"] // 2
    same_core = [[2 * chip + core for chip in range(chips)] for core in range(2)]

    def summed(part):
        return lax.psum_scatter(part, "dp", scatter_dimension=0, axis_index_groups=same_core, tiled=True)

    def step(x, dy, w_gate, w_up, w_down, *moments):
        x, dy = x[0], dy[0]
        layers, d, ff = w_gate.shape

        gate, up, hid0, a0_t = hidden_forward(0, x, w_gate, w_up)
        h1, a1, a1_t = down_forward(0, x, hid0, w_down)
        hid1, dg1, du1 = last_layer(1, a1, dy, w_gate, w_up, w_down)
        gate_up1 = gate_up_gradient(1, 0, ff // (2 * PART), a1_t, dg1, du1)
        hid1, gate_up1 = lax.optimization_barrier((hid1, gate_up1))
        gate_up1 = summed(gate_up1)
        down1 = down_gradient(2, hid1, dy)
        dg1, du1, down1 = lax.optimization_barrier((dg1, du1, down1))
        down1 = summed(down1)
        dh = states_cotangent(1, h1, dy, dg1, du1, w_gate, w_up)
        down0 = down_gradient(3, hid0, dh)
        dh, down0 = lax.optimization_barrier((dh, down0))
        down0 = summed(down0)
        gate_up0 = first_layer_gradient(4, 0, a0_t, dh, gate, up, w_down)
        gate_up0, gate_up1 = lax.optimization_barrier((gate_up0, gate_up1))
        gate_up1, down1 = lax.optimization_barrier((gate_up1, down1))
        down1, down0 = lax.optimization_barrier((down1, down0))
        packs, last, *moments = updated_and_gathered(5, gate_up0, gate_up1, down0, down1, w_gate, w_up, w_down, *moments)
        last = lax.all_gather(last, "dp", tiled=True)
        new_gate, new_up, new_down = placed(packs, layers, d, ff)
        moments[2], moments[5] = copied(moments[2], moments[5])
        new_down = placed_last(new_down, last)
        return new_gate, new_up, new_down, *moments

    sequences = P(("rep", "dp"))
    return jax.shard_map(
        step,
        mesh=mesh,
        in_specs=(sequences, sequences, P(), P(), P(), *[P(None, "dp")] * 6),
        out_specs=(P("rep"), P("rep"), P("rep"), *[P("rep", "dp")] * 6),
        check_vma=False,
    )
```

profile of v0, /device:TPU:97, one launch (start us, length us, event | category | flops | bytes accessed | tf_op | source)
XLA Modules:
  0.0 738.2 jit_solution(14371610527128328318)
XLA Ops:
  7.2 0.1 reduce-scatter.10.cloned.1.call-start
  7.3 62.4 %hidden_forward.1 = (f32[2048,4608]{1,0:T(8,128)}, f32[2048,4608]{1,0:T(8,128)}, bf16[2048,4608]{1,0:T(8,128)(2,1)}, bf16[1152,2048]{1,0:T(8,128)(2,1)}) custom-call(bf16[2048,1152]{1,0:T(8,128)(2,1)} %bitcast.3, bf16[2,1152,4608]{2,1,0:T(8,128)(2,1)} %wg.7, bf16[2,1152,4608]{2,1,0:T(8,128)(2,1)} %wu.7), custom_call_target="tpu_custom_call" | custom-call | flops 43486543872 | bytes 115605504 | tf_op jit(solution)/shard_map/hidden_forward/pallas_call | solution.py:90
  69.6 35.1 %down_forward.1 = (bf16[2048,1152]{1,0:T(8,128)(2,1)}, bf16[2048,1152]{1,0:T(8,128)(2,1)}, bf16[1152,2048]{1,0:T(8,128)(2,1)}) custom-call(bf16[2048,1152]{1,0:T(8,128)(2,1)} %bitcast.4, bf16[2048,4608]{1,0:T(8,128)(2,1)} %get-tuple-element.46.hid, bf16[2,4608,1152]{2,1,0:T(8,128)(2,1)} %wd.5), custom_call_target="tpu_custom_call" | custom-call | flops 21743271936 | bytes 29491200 | tf_op jit(solution)/shard_map/down_forward/pallas_call | solution.py:118
  104.7 84.3 %last_layer.1 = (bf16[2048,4608]{1,0:T(8,128)(2,1)}, bf16[2048,4608]{1,0:T(8,128)(2,1)}, bf16[2048,4608]{1,0:T(8,128)(2,1)}) custom-call(bf16[2048,1152]{1,0:T(8,128)(2,1)} %get-tuple-element.48.a, bf16[2048,1152]{1,0:T(8,128)(2,1)} %bitcast.5, bf16[2,1152,4608]{2,1,0:T(8,128)(2,1)} %wg.7, bf16[2,1152,4608]{2,1,0:T(8,128)(2,1)} %wu.7, bf16[2,4608,1152]{2,1,0:T(8,128)(2,1)} %wd.5), custom_call_target="tpu_custom_call" | custom-call | flops 65229815808 | bytes 88473600 | tf_op jit(solution)/shard_map/last_layer/pallas_call | solution.py:155
  189.0 58.6 %gate_up_gradient_1.1 = bf16[1152,4608]{1,0:T(8,128)(2,1)} custom-call(bf16[1152,2048]{1,0:T(8,128)(2,1)} %get-tuple-element.52.a_t, bf16[2048,4608]{1,0:T(8,128)(2,1)} %get-tuple-element.54.dg0.dg1.dg, bf16[2048,4608]{1,0:T(8,128)(2,1)} %get-tuple-element.54.dg0.dg1.dg, bf16[2048,4608]{1,0:T(8,128)(2,1)} %get-tuple-element.55.du0.du1.du, ...), custom_call_target="tpu_custom_call" | custom-call | flops 43486543872 | bytes 37748736 | tf_op jit(solution)/shard_map/gate_up_gradient_1/pallas_call | solution.py:334
  247.6 0.1 reduce-scatter.10.cloned.1.call-update
  247.7 0.1 reduce-scatter.12.cloned.1.call-start
  247.7 34.5 %down_gradient_2.1 = bf16[2304,1152]{1,0:T(8,128)(2,1)} custom-call(bf16[2048,4608]{1,0:T(8,128)(2,1)} %get-tuple-element.53.hid, bf16[2048,1152]{1,0:T(8,128)(2,1)} %bitcast.6), custom_call_target="tpu_custom_call" | custom-call | flops 21743271936 | bytes 24182784 | tf_op jit(solution)/shard_map/down_gradient_2/pallas_call | solution.py:292
  282.3 0.1 reduce-scatter.12.cloned.1.call-update
  282.3 0.1 reduce-scatter.14.cloned.1.call-start
  282.4 60.6 %states_cotangent.1.dy = bf16[2048,1152]{1,0:T(8,128)(2,1)} custom-call(bf16[2048,1152]{1,0:T(8,128)(2,1)} %get-tuple-element.47.h, bf16[2048,1152]{1,0:T(8,128)(2,1)} %bitcast.7, bf16[2048,4608]{1,0:T(8,128)(2,1)} %get-tuple-element.54.dg0.dg1.dg, bf16[2048,4608]{1,0:T(8,128)(2,1)} %get-tuple-element.55.du0.du1.du, bf16[2,1152,4608]{2,1,0:T(8,128)(2,1)} %wg.7, ...), custom_call_target="tpu_custom_call" | custom-call | flops 43486543872 | bytes 58982400 | tf_op jit(solution)/shard_map/states_cotangent/pallas_call | solution.py:210
  343.0 34.5 %down_gradient_3.1 = bf16[2304,1152]{1,0:T(8,128)(2,1)} custom-call(bf16[2048,4608]{1,0:T(8,128)(2,1)} %get-tuple-element.46.hid, bf16[2048,1152]{1,0:T(8,128)(2,1)} %states_cotangent.1.dy), custom_call_target="tpu_custom_call" | custom-call | flops 21743271936 | bytes 24182784 | tf_op jit(solution)/shard_map/down_gradient_3/pallas_call | solution.py:292
  377.6 0.1 reduce-scatter.14.cloned.1.call-update
  377.7 0.1 all-gather.2.cloned.1.call-start
  377.7 1.2 copy-done.2
  378.9 1.4 copy.29.mg
  380.3 1.4 copy.30.mu
  381.6 1.4 copy.31.vg
  383.0 1.4 copy.32.vu
  384.4 127.4 %first_layer_gradient.1.gu0 = bf16[2,72,2304]{2,1,0:T(8,128)(2,1)} custom-call(bf16[1152,2048]{1,0:T(8,128)(2,1)} %get-tuple-element.45.a_t, bf16[2048,1152]{1,0:T(8,128)(2,1)} %states_cotangent.1.dy, f32[2048,4608]{1,0:T(8,128)} %get-tuple-element.57.g0.g1, f32[2048,4608]{1,0:T(8,128)} %get-tuple-element.57.g0.g1, f32[2048,4608]{1,0:T(8,128)} %get-tuple-element.58.u0.u1, ...), custom_call_target="tpu_custom_call" | custom-call | flops 65229815808 | bytes 75497472 | tf_op jit(solution)/shard_map/first_layer_gradient/pallas_call | solution.py:506
  511.8 0.0 reduce-scatter.10.cloned.1.call-done.gu1
  511.8 0.0 reduce-scatter.12.cloned.1.call-done.d1
  511.9 160.3 %updated_and_gathered.1 = (bf16[4,4,2,2,72,5760]{5,4,3,2,1,0:T(8,128)(2,1)}, bf16[144,1152]{1,0:T(8,128)(2,1)}, f32[2,36,4608]{2,1,0:T(8,128)}, f32[2,36,4608]{2...) custom-call(bf16[2,72,2304]{2,1,0:T(8,128)(2,1)} %first_layer_gradie, ...), custom_call_target="tpu_custom_call" | custom-call | flops 1000000000 | bytes 100000000 | tf_op jit(solution)/shard_map/updated_and_gathered/pallas_call | solution.py:771
  672.2 0.1 all-gather.2.cloned.1.call-update
  672.2 33.6 %placed.1 = (bf16[2,1152,4608]{2,1,0:T(8,128)(2,1)}, bf16[2,1152,4608]{2,1,0:T(8,128)(2,1)}, bf16[2,4608,1152]{2,1,0:T(8,128)(2,1)}) custom-call(bf16[4,4,2,2,72,5760]{5,4,3,2,1,0:T(8,128)(2,1)} %get-tuple-element.68.t), custom_call_target="tpu_custom_call" | custom-call | flops 1 | bytes 106168320 | tf_op jit(solution)/shard_map/placed/pallas_call | solution.py:822
  705.8 2.9 copied.1
  708.7 3.6 copy.33
  712.3 3.5 copy.34
  715.7 2.1 copy.35
  717.8 2.1 copy.36
  719.9 2.9 all-gather.2.cloned.1.call-done.t
  722.9 8.3 %placed_last.1 = bf16[2,4608,1152]{2,1,0:T(8,128)(2,1)} custom-call(bf16[2,4608,1152]{2,1,0:T(8,128)(2,1)} %get-tuple-element.71.down, bf16[4608,1152]{1,0:T(8,128)(2,1)} %all-gather.2.cloned.1.call-done.t), custom_call_target="tpu_custom_call", output_to_operand_aliasing={{}: (0, {})} | custom-call | flops 1 | bytes 21233664 | tf_op jit(solution)/shard_map/placed_last/pallas_call | solution.py:859
  (12 shorter events, 0.0 us)
Async XLA Ops:
  7.2 504.6 %reduce-scatter.10.cloned.1.call-start = ((), (), s32[]{:S(2)}) async-start(), calls=%async_computation.4 | async-start | bytes 11280384
  247.7 264.2 %reduce-scatter.12.cloned.1.call-start = ((), (), s32[]{:S(2)}) async-start(), calls=%async_computation.5 | async-start | bytes 5640192
  282.3 229.5 %reduce-scatter.14.cloned.1.call-start = ((), (), s32[]{:S(2)}) async-start(), calls=%async_computation.6 | async-start | bytes 5640192
  377.6 1.3 copy-start.2
  377.6 2.7 copy-start.3
  377.7 345.2 %all-gather.2.cloned.1.call-start = ((), (), s32[]{:S(2)}) async-start(), calls=%async_computation.3 | async-start | bytes 10948608 | tf_op jit(solution)/shard_map/all_gather | solution.py:901
  378.9 2.7 copy-start.4
  378.9 4.1 copy-start.5
  708.7 7.1 copy-start.1
  708.7 9.2 %copy-start = (f32[2,36,4608]{2,1,0:T(8,128)S(1)}, f32[2,36,4608]{2,1,0:T(8,128)}, u32[]{:S(2)}) copy-start(f32[2,36,4608]{2,1,0:T(8,128)} %get-tuple-element.97) | copy-start | bytes 3981316
Sparse Core Ops, SparseCore 0:
  247.8 86.8 reduce-scatter.9
  338.0 74.4 reduce-scatter.11
  415.8 86.3 reduce-scatter.13
  672.4 50.4 all-gather.1
where the time goes:
time: 746 us; the launch traced here: 738 us
  Pallas kernels  702 us (94%)
  local copies, waits for them, and re-layouts  17.9 us (2%)
  between operations  14.3 us (2%)
    pallas_call x1, Pallas kernels, updated_and_gathered(): call(body, 1000000000.0, 100000000.0, pair_params(number), name='updated_...  160 us
    pallas_call x1, Pallas kernels, first_layer_gradient(): call(body, 12 * tokens * d * PART * n, 16 * tokens * PART * n, pair_param...  127 us
    pallas_call x1, Pallas kernels, last_layer(): call(body, 6 * tokens * d * ff, 6 * tokens * ff + 6 * d * ff, name='last_...  84.3 us
    pallas_call x2, Pallas kernels, down_gradient(): call(body, 2 * tokens * d * ff, 2 * tokens * ff + d * ff, pair_params(num...  69 us
    pallas_call x1, Pallas kernels, hidden_forward(): call(body, 4 * tokens * d * ff, 10 * tokens * ff + 4 * d * ff, name='hidd...  62.4 us
    pallas_call x1, Pallas kernels, states_cotangent(): call(body, 4 * tokens * d * ff, 4 * tokens * ff + 4 * d * ff, name='state...  60.6 us
    pallas_call x1, Pallas kernels, gate_up_gradient(): call(body, 8 * tokens * d * PART * n, 8 * tokens * PART * n, pair_params(...  58.6 us
    pallas_call x1, Pallas kernels, down_forward(): call(body, 2 * tokens * d * ff, 2 * tokens * ff + 2 * d * ff, name='down_...  35.1 us
  transfers between devices with their start and end apart: 4, of which 1 were waited for; matrix products, arithmetic and copies ran while one was open for 2% of the time, Pallas kernels for 40%

commit v1 on v0

--- a/solution.py
+++ b/solution.py
@@ -69,7 +69,9 @@
             def first(i, _):
                 come(i).wait()
                 wide = x_in[rows(i), :].astype(F32)
-                a[rows(i), :] = (wide * row_scale(wide)).astype(BF16)
+                unit = wide * row_scale(wide)
+                a[rows(i), :] = unit.astype(BF16)
+                a_t[:, rows(i)] = unit.T.astype(BF16)
                 chunk(rows(i))
                 return 0
 
@@ -79,10 +81,6 @@
         def _():
             for i in range(n):
                 chunk(slice(i * bm, (i + 1) * bm))
-
-        @pl.when(j == 1)
-        def _():
-            a_t[...] = a[...].T
 
     w_spec = pl.BlockSpec((None, d, bf), lambda j: (layer, 0, j))
     o_spec = pl.BlockSpec((tokens, bf), lambda j: (0, j))
@@ -374,16 +372,16 @@
         here = (x, y)
 
         def transfer(stage, color, way, block):
-            place, slot = lax.rem(block, PLACES), lax.rem(block, SLOTS)
+            place = lax.rem(block, PLACES)
             first, second = color, 1 - color
             columns = slice(color * PART, (color + 1) * PART)
             if stage == 1:
                 far = lax.rem(here[first] + 2, SIDE)
                 part = slice(2 * way, 2 * way + 2)
-                src = sums.at[slot, far, part, :, columns] if color == 0 else sums.at[slot, part, far, :, columns]
+                src = sums.at[place, far, part, :, columns] if color == 0 else sums.at[place, part, far, :, columns]
                 dst = across1.at[color, place, way]
             elif stage == 2:
-                src, dst = pass1.at[color, place, way], got1.at[color, place, way]
+                src, dst = pass1.at[color, lax.rem(block, 2), way], got1.at[color, place, way]
             elif stage == 3:
                 far = lax.rem(here[second] + 2, SIDE)
                 src = total1.at[color, place, far, :, slice(way * mid, (way + 1) * mid)]
@@ -411,9 +409,9 @@
                 device_id_type=pl.DeviceIdType.MESH,
             )
 
-        def of(color, slot, i):
+        def of(color, place, i):
             columns = slice(color * PART, (color + 1) * PART)
-            t = sums[slot, i, :, :, columns] if color == 0 else sums[slot, :, i, :, columns]
+            t = sums[place, i, :, :, columns] if color == 0 else sums[place, :, i, :, columns]
             return t.astype(F32)
 
         def stage(lag, act):
@@ -451,26 +449,26 @@
                     transfer(4, color, way, block).start()
 
         def third(block):
-            place, slot = lax.rem(block, PLACES), lax.rem(block, SLOTS)
+            place = lax.rem(block, PLACES)
             for color in range(2):
                 for way in range(2):
                     transfer(2, color, way, block).wait()
-                t = of(color, slot, here[color]) + got1[color, place, 0].astype(F32) + got1[color, place, 1].astype(F32)
+                t = of(color, place, here[color]) + got1[color, place, 0].astype(F32) + got1[color, place, 1].astype(F32)
                 total1[color, place] = t.astype(BF16)
                 for way in range(2):
                     transfer(3, color, way, block).start()
 
         def second(block):
-            place, slot = lax.rem(block, PLACES), lax.rem(block, SLOTS)
+            place = lax.rem(block, PLACES)
             for color in range(2):
                 for way in range(2):
                     transfer(1, color, way, block).wait()
                 for way in range(2):
-                    t = of(color, slot, lax.rem(here[color] + (1 if way == 0 else SIDE - 1), SIDE))
+                    t = of(color, place, lax.rem(here[color] + (1 if way == 0 else SIDE - 1), SIDE))
                     p = slice(2 * way, 2 * way + 2)
                     q = slice(2 - 2 * way, 4 - 2 * way)
-                    pass1[color, place, way, p] = (t[p] + across1[color, place, way].astype(F32)).astype(BF16)
-                    pass1[color, place, way, q] = t[q].astype(BF16)
+                    pass1[color, lax.rem(block, 2), way, p] = (t[p] + across1[color, place, way].astype(F32)).astype(BF16)
+                    pass1[color, lax.rem(block, 2), way, q] = t[q].astype(BF16)
                     transfer(2, color, way, block).start()
 
         def first(block):
@@ -479,7 +477,7 @@
             for k in range(SIDE**2):
                 r = slice(k * rows, (k + 1) * rows)
                 t = made[slot, core, r, :].astype(F32) + came[place, r, :].astype(F32)
-                sums[slot, k // SIDE, k % SIDE] = t.astype(BF16)
+                sums[place, k // SIDE, k % SIDE] = t.astype(BF16)
             for color in range(2):
                 for way in range(2):
                     transfer(1, color, way, block).start()
@@ -494,10 +492,10 @@
                 made[slot, h, :, PART:] = dot(a_t[...], du[h]).astype(BF16)
             swap(block).start()
 
-        stage(6, last)
-        stage(5, fourth)
-        stage(4, third)
-        stage(3, second)
+        stage(8, last)
+        stage(7, fourth)
+        stage(6, third)
+        stage(4, second)
         stage(2, first)
         stage(0, make)
 
@@ -509,18 +507,18 @@
         16 * tokens * PART * n,
         pair_params(number),
         name="first_layer_gradient",
-        grid=(n + 6,),
+        grid=(n + 8,),
         in_specs=[whole((d, tokens)), whole((tokens, d)), *t_specs, *t_specs, *halves_specs((None, PART, d), 0, n, half, layer, True)],
-        out_specs=pl.BlockSpec((2, rows, PART), lambda j: (0, 0, jnp.maximum(j - 6, 0))),
+        out_specs=pl.BlockSpec((2, rows, PART), lambda j: (0, 0, jnp.maximum(j - 8, 0))),
         out_shape=jax.ShapeDtypeStruct((2, rows, PART * n), BF16),
         scratch_shapes=[
             pltpu.VMEM((2, tokens, PART), BF16),
             pltpu.VMEM((2, tokens, PART), BF16),
             pltpu.VMEM((SLOTS, 2, d, 2 * PART), BF16),
             pltpu.VMEM((PLACES, d, 2 * PART), BF16),
-            pltpu.VMEM((SLOTS, SIDE, SIDE, rows, 2 * PART), BF16),
+            pltpu.VMEM((PLACES, SIDE, SIDE, rows, 2 * PART), BF16),
             pltpu.VMEM((2, PLACES, 2, SIDE // 2, rows, PART), BF16),
-            pltpu.VMEM((2, PLACES, 2, *block), BF16),
+            pltpu.VMEM((2, 2, 2, *block), BF16),
             pltpu.VMEM((2, PLACES, 2, *block), BF16),
             pltpu.VMEM((2, PLACES, *block), BF16),
             pltpu.VMEM((2, PLACES, 2, rows, mid), BF16),
@@ -559,7 +557,7 @@
         moments = (mg, mu, vg, vu)
         new_moments = (nmg, nmu, nvg, nvu)
         loads = [
-            *[(t.at[:, :, mine], mom.at[k, core]) for k, t in enumerate(moments)],
+            *[(t.at[:, l, mine], mom.at[k, core, l]) for k, t in enumerate(moments) for l in range(layers)],
             (md, mom_d.at[0]),
             (vd, mom_d.at[1]),
             (wg.at[:, pl.ds(pl.multiple_of(chip * rows, 8), rows), mine], w_gu.at[0]),
@@ -613,7 +611,7 @@
             )
 
         lax.fori_loop(1, n, lambda i, _: (size(i).start(), 0)[1], 0)
-        swaps = [swap(t.at[:, :, theirs], mom.at[k, core], k) for k, t in enumerate(moments)]
+        swaps = [swap(t.at[:, l, theirs], mom.at[k, core, l], k * layers + l) for k, t in enumerate(moments) for l in range(layers)]
         for copy in swaps:
             copy.start()
         for copy in loads:
@@ -720,13 +718,13 @@
         spare[...] = step_down(1, slice(0, own_rows), d1)
 
         stores = [
-            *[(mom.at[k, core], t.at[:, :, mine]) for k, t in enumerate(new_moments)],
+            *[(mom.at[k, core, l], t.at[:, l, mine]) for k, t in enumerate(new_moments) for l in range(layers)],
             (mom_d.at[0], nmd),
             (mom_d.at[1], nvd),
             (spare, wd1),
         ]
         stores = [pltpu.make_async_copy(a, b, load.at[2 + k]) for k, (a, b) in enumerate(stores)]
-        backs = [swap(mom.at[k, 1 - core], t.at[:, :, mine], 4 + k) for k, t in enumerate(new_moments)]
+        backs = [swap(mom.at[k, 1 - core, l], t.at[:, l, mine], 8 + k * layers + l) for k, t in enumerate(new_moments) for l in range(layers)]
         for copy in (*stores, *backs):
             copy.start()
 
@@ -766,9 +764,10 @@
         for copy in (*kept, *stores, *backs):
             copy.wait()
 
+    m_gate, m_up, v_gate, v_up = (t.transpose(1, 0, 2) for t in (m_gate, m_up, v_gate, v_up))
     anywhere = pl.BlockSpec(memory_space=pl.ANY)
     vmem = pl.BlockSpec(memory_space=pltpu.VMEM)
-    return call(
+    packs, last, *moments = call(
         body,
         1e9,
         1e8,
@@ -790,15 +789,16 @@
             pltpu.VMEM((own_rows, d), BF16),
             pltpu.VMEM((8, 128), F32),
             pltpu.VMEM((n, 8, 128), F32),
-            pltpu.SemaphoreType.DMA((9,)),
-            pltpu.SemaphoreType.DMA((8,)),
-            pltpu.SemaphoreType.DMA((8,)),
+            pltpu.SemaphoreType.DMA((13,)),
+            pltpu.SemaphoreType.DMA((16,)),
+            pltpu.SemaphoreType.DMA((16,)),
             pltpu.SemaphoreType.DMA((n,)),
             pltpu.SemaphoreType.DMA((n,)),
             pltpu.SemaphoreType.DMA((124,)),
             pltpu.SemaphoreType.DMA((124,)),
         ],
     )(gate_up0, gate_up1, down0, down1, w_gate, w_up, w_down, m_gate, m_up, m_down, v_gate, v_up, v_down)
+    return packs, last, *moments
 
 
 def placed(packs, layers, d, ff):
@@ -832,17 +832,19 @@
 
 
 def copied(*arrays):
+    steps = 4
+
     def body(*refs):
         for a, b in zip(refs[: len(arrays)], refs[len(arrays) :], strict=True):
             b[...] = a[...]
 
-    specs = [pl.BlockSpec((1, *t.shape[1:]), lambda i: (i, 0, 0)) for t in arrays]
+    specs = [pl.BlockSpec((t.shape[0] // steps, *t.shape[1:]), lambda i: (i, 0, 0)) for t in arrays]
     return call(
         body,
         1,
         sum(8 * t.size for t in arrays),
         name="copied",
-        grid=(arrays[0].shape[0],),
+        grid=(steps,),
         in_specs=specs,
         out_specs=specs,
         out_shape=[jax.ShapeDtypeStruct(t.shape, t.dtype) for t in arrays],
@@ -900,7 +902,11 @@
         packs, last, *moments = updated_and_gathered(5, gate_up0, gate_up1, down0, down1, w_gate, w_up, w_down, *moments)
         last = lax.all_gather(last, "dp", tiled=True)
         new_gate, new_up, new_down = placed(packs, layers, d, ff)
-        moments[2], moments[5] = copied(moments[2], moments[5])
+        down_moments = [t.reshape(-1, t.shape[1] // 2, d) for t in moments[2::3]]
+        moments = copied(*(t for k, t in enumerate(moments) if k % 3 < 2), *down_moments)
+        down_moments = [t.reshape(layers, -1, d) for t in moments[4:]]
+        moments = [t.transpose(1, 0, 2) for t in moments[:4]]
+        moments = [*moments[:2], down_moments[0], *moments[2:], down_moments[1]]
         new_down = placed_last(new_down, last)
         return new_gate, new_up, new_down, *moments
 

time: 746 us -> 738 us (0.989)
  local copies, waits for them, and re-layouts: 17.9 us -> 0 us
    unnamed x20 -> x0, local copies, waits for them, and re-layouts: 17.9 us -> none
  transfers between devices with their start and end apart: 4 -> 4, of which waited for: 1 -> 1; matrix products, arithmetic and copies ran while one was open for 2% -> 0% of each run, Pallas kernels for 40% -> 41%
where the time goes in v1:
time: 738 us; the launch traced here: 731 us
  Pallas kernels  706 us (96%)
  between operations  14.4 us (2%)
  waiting for transfers between devices  10.6 us (1%)
    pallas_call x1, Pallas kernels, updated_and_gathered(): call(body, 1000000000.0, 100000000.0, pair_params(number), name='updated_...  158 us
    pallas_call x1, Pallas kernels, first_layer_gradient(): call(body, 12 * tokens * d * PART * n, 16 * tokens * PART * n, pair_param...  131 us
    pallas_call x1, Pallas kernels, last_layer(): call(body, 6 * tokens * d * ff, 6 * tokens * ff + 6 * d * ff, name='last_...  84.4 us
    pallas_call x2, Pallas kernels, down_gradient(): call(body, 2 * tokens * d * ff, 2 * tokens * ff + d * ff, pair_params(num...  69.1 us
    pallas_call x1, Pallas kernels, hidden_forward(): call(body, 4 * tokens * d * ff, 10 * tokens * ff + 4 * d * ff, name='hidd...  61.2 us
    pallas_call x1, Pallas kernels, states_cotangent(): call(body, 4 * tokens * d * ff, 4 * tokens * ff + 4 * d * ff, name='state...  60.7 us
    pallas_call x1, Pallas kernels, gate_up_gradient(): call(body, 8 * tokens * d * PART * n, 8 * tokens * PART * n, pair_params(...  58.3 us
    pallas_call x1, Pallas kernels, down_forward(): call(body, 2 * tokens * d * ff, 2 * tokens * ff + 2 * d * ff, name='down_...  35.1 us
  transfers between devices with their start and end apart: 4, of which 1 were waited for; matrix products, arithmetic and copies ran while one was open for 0% of the time, Pallas kernels for 41%

profile of v1, /device:TPU:97, one launch (start us, length us, event | category | flops | bytes accessed | tf_op | source)
XLA Modules:
  0.0 730.9 jit_solution(5651254212202647919)
XLA Ops:
  7.2 0.1 reduce-scatter.10.cloned.1.call-start
  7.3 61.2 %hidden_forward.1 = (f32[2048,4608]{1,0:T(8,128)}, f32[2048,4608]{1,0:T(8,128)}, bf16[2048,4608]{1,0:T(8,128)(2,1)}, bf16[1152,2048]{1,0:T(8,128)(2,1)}) custom-call(bf16[2048,1152]{1,0:T(8,128)(2,1)} %bitcast.21, bf16[2,1152,4608]{2,1,0:T(8,128)(2,1)} %wg.7, bf16[2,1152,4608]{2,1,0:T(8,128)(2,1)} %wu.7), custom_call_target="tpu_custom_call" | custom-call | flops 43486543872 | bytes 115605504 | tf_op jit(solution)/shard_map/hidden_forward/pallas_call | solution.py:88
  68.5 35.1 %down_forward.1 = (bf16[2048,1152]{1,0:T(8,128)(2,1)}, bf16[2048,1152]{1,0:T(8,128)(2,1)}, bf16[1152,2048]{1,0:T(8,128)(2,1)}) custom-call(bf16[2048,1152]{1,0:T(8,128)(2,1)} %bitcast.22, bf16[2048,4608]{1,0:T(8,128)(2,1)} %get-tuple-element.50.hid, bf16[2,4608,1152]{2,1,0:T(8,128)(2,1)} %wd.5), custom_call_target="tpu_custom_call" | custom-call | flops 21743271936 | bytes 29491200 | tf_op jit(solution)/shard_map/down_forward/pallas_call | solution.py:116
  103.6 84.4 %last_layer.1 = (bf16[2048,4608]{1,0:T(8,128)(2,1)}, bf16[2048,4608]{1,0:T(8,128)(2,1)}, bf16[2048,4608]{1,0:T(8,128)(2,1)}) custom-call(bf16[2048,1152]{1,0:T(8,128)(2,1)} %get-tuple-element.52.a, bf16[2048,1152]{1,0:T(8,128)(2,1)} %bitcast.23, bf16[2,1152,4608]{2,1,0:T(8,128)(2,1)} %wg.7, bf16[2,1152,4608]{2,1,0:T(8,128)(2,1)} %wu.7, bf16[2,4608,1152]{2,1,0:T(8,128)(2,1)} %wd.5), custom_call_target="tpu_custom_call" | custom-call | flops 65229815808 | bytes 88473600 | tf_op jit(solution)/shard_map/last_layer/pallas_call | solution.py:153
  187.9 58.3 %gate_up_gradient_1.1 = bf16[1152,4608]{1,0:T(8,128)(2,1)} custom-call(bf16[1152,2048]{1,0:T(8,128)(2,1)} %get-tuple-element.56.a_t, bf16[2048,4608]{1,0:T(8,128)(2,1)} %get-tuple-element.58.dg0.dg1.dg, bf16[2048,4608]{1,0:T(8,128)(2,1)} %get-tuple-element.58.dg0.dg1.dg, bf16[2048,4608]{1,0:T(8,128)(2,1)} %get-tuple-element.59.du0.du1.du, ...), custom_call_target="tpu_custom_call" | custom-call | flops 43486543872 | bytes 37748736 | tf_op jit(solution)/shard_map/gate_up_gradient_1/pallas_call | solution.py:332
  246.3 0.1 reduce-scatter.10.cloned.1.call-update
  246.3 0.1 reduce-scatter.12.cloned.1.call-start
  246.4 34.5 %down_gradient_2.1 = bf16[2304,1152]{1,0:T(8,128)(2,1)} custom-call(bf16[2048,4608]{1,0:T(8,128)(2,1)} %get-tuple-element.57.hid, bf16[2048,1152]{1,0:T(8,128)(2,1)} %bitcast.24), custom_call_target="tpu_custom_call" | custom-call | flops 21743271936 | bytes 24182784 | tf_op jit(solution)/shard_map/down_gradient_2/pallas_call | solution.py:290
  280.9 0.1 reduce-scatter.12.cloned.1.call-update
  281.0 0.1 reduce-scatter.14.cloned.1.call-start
  281.1 60.7 %states_cotangent.1.dy = bf16[2048,1152]{1,0:T(8,128)(2,1)} custom-call(bf16[2048,1152]{1,0:T(8,128)(2,1)} %get-tuple-element.51.h, bf16[2048,1152]{1,0:T(8,128)(2,1)} %bitcast.25, bf16[2048,4608]{1,0:T(8,128)(2,1)} %get-tuple-element.58.dg0.dg1.dg, bf16[2048,4608]{1,0:T(8,128)(2,1)} %get-tuple-element.59.du0.du1.du, bf16[2,1152,4608]{2,1,0:T(8,128)(2,1)} %wg.7, ...), custom_call_target="tpu_custom_call" | custom-call | flops 43486543872 | bytes 58982400 | tf_op jit(solution)/shard_map/states_cotangent/pallas_call | solution.py:208
  341.7 34.6 %down_gradient_3.1 = bf16[2304,1152]{1,0:T(8,128)(2,1)} custom-call(bf16[2048,4608]{1,0:T(8,128)(2,1)} %get-tuple-element.50.hid, bf16[2048,1152]{1,0:T(8,128)(2,1)} %states_cotangent.1.dy), custom_call_target="tpu_custom_call" | custom-call | flops 21743271936 | bytes 24182784 | tf_op jit(solution)/shard_map/down_gradient_3/pallas_call | solution.py:290
  376.3 0.1 reduce-scatter.14.cloned.1.call-update
  376.4 0.1 all-gather.2.cloned.1.call-start
  376.4 130.7 %first_layer_gradient.1.gu0 = bf16[2,72,2304]{2,1,0:T(8,128)(2,1)} custom-call(bf16[1152,2048]{1,0:T(8,128)(2,1)} %get-tuple-element.49.a_t, bf16[2048,1152]{1,0:T(8,128)(2,1)} %states_cotangent.1.dy, f32[2048,4608]{1,0:T(8,128)} %get-tuple-element.61.g0.g1, f32[2048,4608]{1,0:T(8,128)} %get-tuple-element.61.g0.g1, f32[2048,4608]{1,0:T(8,128)} %get-tuple-element.62.u0.u1, ...), custom_call_target="tpu_custom_call" | custom-call | flops 65229815808 | bytes 75497472 | tf_op jit(solution)/shard_map/first_layer_gradient/pallas_call | solution.py:504
  507.1 0.0 reduce-scatter.10.cloned.1.call-done.gu1
  507.2 0.0 reduce-scatter.12.cloned.1.call-done.d1
  507.2 0.0 reduce-scatter.14.cloned.1.call-done.d0
  507.2 157.7 %updated_and_gathered.1 = (bf16[4,4,2,2,72,5760]{5,4,3,2,1,0:T(8,128)(2,1)}, bf16[144,1152]{1,0:T(8,128)(2,1)}, f32[36,2,4608]{2,1,0:T(2,128)}, f32[36,2,4608]{2...) custom-call(bf16[2,72,2304]{2,1,0:T(8,128)(2,1)} %first_layer_gradie, ...), custom_call_target="tpu_custom_call" | custom-call | flops 1000000000 | bytes 100000000 | tf_op jit(solution)/shard_map/updated_and_gathered/pallas_call | solution.py:770
  664.9 0.1 all-gather.2.cloned.1.call-update
  665.0 33.6 %placed.1 = (bf16[2,1152,4608]{2,1,0:T(8,128)(2,1)}, bf16[2,1152,4608]{2,1,0:T(8,128)(2,1)}, bf16[2,4608,1152]{2,1,0:T(8,128)(2,1)}) custom-call(bf16[4,4,2,2,72,5760]{5,4,3,2,1,0:T(8,128)(2,1)} %get-tuple-element.72.t), custom_call_target="tpu_custom_call" | custom-call | flops 1 | bytes 106168320 | tf_op jit(solution)/shard_map/placed/pallas_call | solution.py:822
  698.5 6.7 copied.1
  705.2 10.3 %all-gather.2.cloned.1.call-done.t = bf16[4608,1152]{1,0:T(8,128)(2,1)} async-done(((bf16[144,1152]{1,0:T(8,128)(2,1)}), bf16[4608,1152]{1,0:T(8,128)(2,1)}) %all-gather.2.cloned.1.call-update) | async-done | bytes 10616848 | tf_op jit(solution)/shard_map/all_gather | solution.py:903
  715.5 8.3 %placed_last.1 = bf16[2,4608,1152]{2,1,0:T(8,128)(2,1)} custom-call(bf16[2,4608,1152]{2,1,0:T(8,128)(2,1)} %get-tuple-element.75.down, bf16[4608,1152]{1,0:T(8,128)(2,1)} %all-gather.2.cloned.1.call-done.t), custom_call_target="tpu_custom_call", output_to_operand_aliasing={{}: (0, {})} | custom-call | flops 1 | bytes 21233664 | tf_op jit(solution)/shard_map/placed_last/pallas_call | solution.py:861
Async XLA Ops:
  7.2 500.0 %reduce-scatter.10.cloned.1.call-start = ((), (), s32[]{:S(2)}) async-start(), calls=%async_computation.4 | async-start | bytes 11280384
  246.3 260.8 %reduce-scatter.12.cloned.1.call-start = ((), (), s32[]{:S(2)}) async-start(), calls=%async_computation.5 | async-start | bytes 5640192
  281.0 226.2 %reduce-scatter.14.cloned.1.call-start = ((), (), s32[]{:S(2)}) async-start(), calls=%async_computation.6 | async-start | bytes 5640192
  376.4 339.1 %all-gather.2.cloned.1.call-start = ((), (), s32[]{:S(2)}) async-start(), calls=%async_computation.3 | async-start | bytes 10948608 | tf_op jit(solution)/shard_map/all_gather | solution.py:903
Sparse Core Ops, SparseCore 0:
  246.5 86.8 reduce-scatter.9
  336.6 75.5 reduce-scatter.11
  415.6 87.3 reduce-scatter.13
  665.1 50.3 all-gather.1

commit v2 on v1

--- a/solution.py
+++ b/solution.py
@@ -230,7 +230,7 @@
     ]
 
 
-def pair_step(n, make, out, made, came, sent, arrived):
+def pair_step(n, make, put, made, came, sent, arrived):
     j = pl.program_id(0)
     me = lax.axis_index("dp")
     core = lax.rem(me, 2)
@@ -257,7 +257,7 @@
     def _():
         transfer(j - 2).wait()
         own = made[lax.rem(j - 2, SLOTS), core]
-        out[...] = (own.astype(F32) + came[lax.rem(j - 2, ARRIVALS)].astype(F32)).astype(BF16)
+        put(own.astype(F32) + came[lax.rem(j - 2, ARRIVALS)].astype(F32))
 
     @pl.when(j < n)
     def _():
@@ -269,7 +269,7 @@
     return {"collective_id": number, "has_side_effects": True}
 
 
-def down_gradient(number, hid, dy):
+def down_gradient(number, hid, dy, joint=None):
     tokens, ff = hid.shape
     d = dy.shape[-1]
     chips = lax.axis_size("dp") // 2
@@ -277,7 +277,9 @@
     bf = 1152
     n, per = ff // bf, bf // (2 * own)
 
-    def body(hid, dy, out, *scratch):
+    def body(hid, dy, *rest):
+        out, *scratch = rest[0 if joint is None else 1 :]
+
         def make(slot):
             block = dot(hid[...], dy[...], TN)
             for i in range(per):
@@ -285,8 +287,23 @@
                     at = (2 * i + half) * own
                     slot[half, i * own : (i + 1) * own, :] = block[at : at + own].astype(BF16)
 
-        pair_step(n, make, out, *scratch)
-
+        def put(total):
+            if joint is None:
+                out[...] = total.astype(BF16)
+            else:
+                for i in range(per):
+                    for half in range(2):
+                        at = i * own + half * (own // 2)
+                        out[i, :, half * d : (half + 1) * d] = total[at : at + own // 2].astype(BF16)
+
+        pair_step(n, make, put, *scratch)
+
+    if joint is None:
+        more, out_shape = [], jax.ShapeDtypeStruct((ff // 2, d), BF16)
+        out_spec = pl.BlockSpec((bf // 2, d), lambda j: (jnp.maximum(j - 2, 0), 0))
+    else:
+        more, out_shape = [joint], jax.ShapeDtypeStruct(joint.shape, BF16)
+        out_spec = pl.BlockSpec((per, None, own // 2, 2 * d), lambda j: (jnp.maximum(j - 2, 0), 2, 0, 0))
     return call(
         body,
         2 * tokens * d * ff,
@@ -294,11 +311,16 @@
         pair_params(number),
         name=f"down_gradient_{number}",
         grid=(n + 2,),
-        in_specs=[pl.BlockSpec((tokens, bf), lambda j: (0, jnp.minimum(j, n - 1))), whole((tokens, d))],
-        out_specs=pl.BlockSpec((bf // 2, d), lambda j: (jnp.maximum(j - 2, 0), 0)),
-        out_shape=jax.ShapeDtypeStruct((ff // 2, d), BF16),
+        in_specs=[
+            pl.BlockSpec((tokens, bf), lambda j: (0, jnp.minimum(j, n - 1))),
+            whole((tokens, d)),
+            *[pl.BlockSpec(memory_space=pl.ANY) for _ in more],
+        ],
+        out_specs=out_spec,
+        out_shape=out_shape,
         scratch_shapes=pair_scratch(bf // 2, d),
-    )(hid, dy)
+        input_output_aliases={2: 0} if more else {},
+    )(hid, dy, *more)
 
 
 PART = 256
@@ -316,9 +338,12 @@
     return [spec(0), spec(1)]
 
 
-def gate_up_gradient(number, first, n, a_t, dg, du):
+def gate_up_gradient(number, a_t, dg, du):
     d, tokens = a_t.shape
     half = dg.shape[-1] // (2 * PART)
+    n = half
+    chips = lax.axis_size("dp") // 2
+    rows = d // chips
 
     def body(a_t, dg0, dg1, du0, du1, out, *scratch):
         def make(slot):
@@ -326,9 +351,14 @@
                 slot[h, :, :PART] = dot(a_t[...], dg[...]).astype(BF16)
                 slot[h, :, PART:] = dot(a_t[...], du[...]).astype(BF16)
 
-        pair_step(n, make, out, *scratch)
-
-    t_specs = halves_specs((tokens, PART), first, n, half)
+        def put(total):
+            for k in range(chips):
+                for i in range(2):
+                    out[k, i] = total[k * rows : (k + 1) * rows, i * PART : (i + 1) * PART].astype(BF16)
+
+        pair_step(n, make, put, *scratch)
+
+    t_specs = halves_specs((tokens, PART), 0, n, half)
     return call(
         body,
         8 * tokens * d * PART * n,
@@ -337,8 +367,8 @@
         name=f"gate_up_gradient_{number}",
         grid=(n + 2,),
         in_specs=[whole((d, tokens)), *t_specs, *t_specs],
-        out_specs=pl.BlockSpec((d, 2 * PART), lambda j: (0, jnp.maximum(j - 2, 0))),
-        out_shape=jax.ShapeDtypeStruct((d, 2 * PART * n), BF16),
+        out_specs=pl.BlockSpec((chips, 2, rows, PART), lambda j: (0, 0, 0, jnp.maximum(j - 2, 0))),
+        out_shape=jax.ShapeDtypeStruct((chips, 3, rows, PART * n), BF16),
         scratch_shapes=pair_scratch(d, 2 * PART),
     )(a_t, dg, dg, du, du)
 
@@ -532,7 +562,7 @@
     )(a_t, dy, gate, gate, up, up, w_down, w_down)
 
 
-def updated_and_gathered(number, gate_up0, gate_up1, down0, down1, w_gate, w_up, w_down, m_gate, m_up, m_down, v_gate, v_up, v_down):
+def updated_and_gathered(number, gate_up0, down0, last_layer, w_gate, w_up, w_down, m_gate, m_up, m_down, v_gate, v_up, v_down):
     n = lax.axis_size("dp")
     layers, d, ff = w_gate.shape
     rows, half = gate_up0.shape[1:]
@@ -544,7 +574,7 @@
     parts = (slice(0, cut), slice(cut, width))
     plan = []
 
-    def body(gu0, gu1, d0, d1, wg, wu, wd, mg, mu, md, vg, vu, vd, ag, wd1, nmg, nmu, nmd, nvg, nvu, nvd,
+    def body(gu0, d0, gu1, wg, wu, wd, mg, mu, md, vg, vu, vd, ag, wd1, nmg, nmu, nmd, nvg, nvu, nvd,
              w_gu, w_d, mom, mom_d, packs, spare, tile, tiles, load, swap_s, swap_r, norm_s, norm_r, sent, arrived):
         me = lax.axis_index("dp")
         core = lax.rem(me, 2)
@@ -583,12 +613,10 @@
 
         def squares(k, total):
             at = pl.ds(pl.multiple_of(k * PART, PART), PART)
-            both = pl.ds(pl.multiple_of(k * 2 * PART, PART), 2 * PART)
-            two = square(gu1[:, both])
-            return total + square(gu0[0, :, at]) + square(gu0[1, :, at]) + two[:, :PART] + two[:, PART:]
+            return total + sum(square(gu0[i, :, at]) for i in range(2)) + sum(square(gu1[i, :, at]) for i in range(3))
 
         total = lax.fori_loop(0, steps, squares, jnp.zeros((8, PART), F32))
-        downs = square(d0[...]) + square(d1[...])
+        downs = square(d0[...])
         total = total[:, :128] + total[:, 128:] + sum(downs[:, k * 128 : (k + 1) * 128] for k in range(d // 128))
         tile[...] = total
         tiles[0] = total
@@ -634,11 +662,7 @@
 
                 def columns(k, _, gu=gu):
                     at = pl.ds(pl.multiple_of(k * PART, PART), PART)
-                    if layer == 0:
-                        g = gu0[gu, :, at]
-                    else:
-                        g = gu1[:, pl.ds(pl.multiple_of((2 * k + gu) * PART, PART), PART)]
-                    g = g.astype(F32)
+                    g = (gu0, gu1)[layer][gu, :, at].astype(F32)
                     w = w_gu[gu, layer, :, at].astype(F32)
                     new = []
                     for r in range(2):
@@ -653,7 +677,7 @@
                 lax.fori_loop(0, steps, columns, 0)
 
         def step_down(layer, p, g):
-            new, m, v = adamw(w_d[layer, p, :].astype(F32), mom_d[0, layer, p, :], mom_d[1, layer, p, :], g[p, :].astype(F32))
+            new, m, v = adamw(w_d[layer, p, :].astype(F32), mom_d[0, layer, p, :], mom_d[1, layer, p, :], g.astype(F32))
             mom_d[0, layer, p, :] = m
             mom_d[1, layer, p, :] = v
             return new.astype(BF16)
@@ -710,12 +734,14 @@
             return copy
 
         step_gate_up(0)
-        packs[0, :, 2 * half :] = step_down(0, slice(0, rows), d0)
+        packs[0, :, 2 * half :] = step_down(0, slice(0, rows), d0[:rows])
         kept = [own(0)]
         step_gate_up(1)
-        packs[1, :, 2 * half :] = step_down(0, slice(rows, 2 * rows), d0)
+        packs[1, :, 2 * half :] = step_down(0, slice(rows, 2 * rows), d0[rows:])
         kept.append(own(1))
-        spare[...] = step_down(1, slice(0, own_rows), d1)
+        for i in range(2):
+            p = slice(i * rows, (i + 1) * rows)
+            spare[p] = step_down(1, p, gu1[2, :, i * d : (i + 1) * d])
 
         stores = [
             *[(mom.at[k, core, l], t.at[:, l, mine]) for k, t in enumerate(new_moments) for l in range(layers)],
@@ -773,7 +799,7 @@
         1e8,
         pair_params(number),
         name="updated_and_gathered",
-        in_specs=[vmem] * 4 + [anywhere] * 9,
+        in_specs=[vmem] * 3 + [anywhere] * 9,
         out_specs=[anywhere] * 8,
         out_shape=[
             jax.ShapeDtypeStruct((SIDE, SIDE, 2, 2, rows, width), BF16),
@@ -797,7 +823,7 @@
             pltpu.SemaphoreType.DMA((124,)),
             pltpu.SemaphoreType.DMA((124,)),
         ],
-    )(gate_up0, gate_up1, down0, down1, w_gate, w_up, w_down, m_gate, m_up, m_down, v_gate, v_up, v_down)
+    )(gate_up0, down0, last_layer, w_gate, w_up, w_down, m_gate, m_up, m_down, v_gate, v_up, v_down)
     return packs, last, *moments
 
 
@@ -885,21 +911,18 @@
         gate, up, hid0, a0_t = hidden_forward(0, x, w_gate, w_up)
         h1, a1, a1_t = down_forward(0, x, hid0, w_down)
         hid1, dg1, du1 = last_layer(1, a1, dy, w_gate, w_up, w_down)
-        gate_up1 = gate_up_gradient(1, 0, ff // (2 * PART), a1_t, dg1, du1)
-        hid1, gate_up1 = lax.optimization_barrier((hid1, gate_up1))
-        gate_up1 = summed(gate_up1)
-        down1 = down_gradient(2, hid1, dy)
-        dg1, du1, down1 = lax.optimization_barrier((dg1, du1, down1))
-        down1 = summed(down1)
+        joint = gate_up_gradient(1, a1_t, dg1, du1)
+        joint = down_gradient(2, hid1, dy, joint)
+        dg1, du1, joint = lax.optimization_barrier((dg1, du1, joint))
+        of_last = summed(joint.reshape(-1, joint.shape[-1])).reshape(joint.shape[1:])
         dh = states_cotangent(1, h1, dy, dg1, du1, w_gate, w_up)
         down0 = down_gradient(3, hid0, dh)
         dh, down0 = lax.optimization_barrier((dh, down0))
         down0 = summed(down0)
         gate_up0 = first_layer_gradient(4, 0, a0_t, dh, gate, up, w_down)
-        gate_up0, gate_up1 = lax.optimization_barrier((gate_up0, gate_up1))
-        gate_up1, down1 = lax.optimization_barrier((gate_up1, down1))
-        down1, down0 = lax.optimization_barrier((down1, down0))
-        packs, last, *moments = updated_and_gathered(5, gate_up0, gate_up1, down0, down1, w_gate, w_up, w_down, *moments)
+        gate_up0, of_last = lax.optimization_barrier((gate_up0, of_last))
+        of_last, down0 = lax.optimization_barrier((of_last, down0))
+        packs, last, *moments = updated_and_gathered(5, gate_up0, down0, of_last, w_gate, w_up, w_down, *moments)
         last = lax.all_gather(last, "dp", tiled=True)
         new_gate, new_up, new_down = placed(packs, layers, d, ff)
         down_moments = [t.reshape(-1, t.shape[1] // 2, d) for t in moments[2::3]]

time: 738 us -> 731 us (level)
    pallas_call x1, Pallas kernels: 131 us -> 123 us  [first_layer_gradient(): call(body, 12 * tokens * d * PART * n, 16 * tokens * PART * n, pair_param...]
  transfers between devices with their start and end apart: 4 -> 3, of which waited for: 1 -> 1; matrix products, arithmetic and copies ran while one was open for 0% -> 0% of each run, Pallas kernels for 41% -> 36%
where the time goes in v2:
time: 731 us; the launch traced here: 724 us
  Pallas kernels  699 us (96%)
  between operations  14.4 us (2%)
  waiting for transfers between devices  10.5 us (1%)
    pallas_call x1, Pallas kernels, updated_and_gathered(): call(body, 1000000000.0, 100000000.0, pair_params(number), name='updated_...  159 us
    pallas_call x1, Pallas kernels, first_layer_gradient(): call(body, 12 * tokens * d * PART * n, 16 * tokens * PART * n, pair_param...  123 us
    pallas_call x1, Pallas kernels, last_layer(): call(body, 6 * tokens * d * ff, 6 * tokens * ff + 6 * d * ff, name='last_...  84.4 us
    pallas_call x2, Pallas kernels, down_gradient(): call(body, 2 * tokens * d * ff, 2 * tokens * ff + d * ff, pair_params(num...  69.1 us
    pallas_call x1, Pallas kernels, hidden_forward(): call(body, 4 * tokens * d * ff, 10 * tokens * ff + 4 * d * ff, name='hidd...  61.2 us
    pallas_call x1, Pallas kernels, states_cotangent(): call(body, 4 * tokens * d * ff, 4 * tokens * ff + 4 * d * ff, name='state...  60.7 us
    pallas_call x1, Pallas kernels, gate_up_gradient(): call(body, 8 * tokens * d * PART * n, 8 * tokens * PART * n, pair_params(...  58.4 us
    pallas_call x1, Pallas kernels, down_forward(): call(body, 2 * tokens * d * ff, 2 * tokens * ff + 2 * d * ff, name='down_...  35.1 us
  transfers between devices with their start and end apart: 3, of which 1 were waited for; matrix products, arithmetic and copies ran while one was open for 0% of the time, Pallas kernels for 36%

profile of v2, /device:TPU:97, one launch (start us, length us, event | category | flops | bytes accessed | tf_op | source)
XLA Modules:
  0.0 724.2 jit_solution(14102956428138948069)
XLA Ops:
  7.2 0.1 reduce-scatter.7.cloned.1.call-start
  7.3 61.2 %hidden_forward.1 = (f32[2048,4608]{1,0:T(8,128)}, f32[2048,4608]{1,0:T(8,128)}, bf16[2048,4608]{1,0:T(8,128)(2,1)}, bf16[1152,2048]{1,0:T(8,128)(2,1)}) custom-call(bf16[2048,1152]{1,0:T(8,128)(2,1)} %bitcast.25, bf16[2,1152,4608]{2,1,0:T(8,128)(2,1)} %wg.7, bf16[2,1152,4608]{2,1,0:T(8,128)(2,1)} %wu.7), custom_call_target="tpu_custom_call" | custom-call | flops 43486543872 | bytes 115605504 | tf_op jit(solution)/shard_map/hidden_forward/pallas_call | solution.py:88
  68.5 35.1 %down_forward.1 = (bf16[2048,1152]{1,0:T(8,128)(2,1)}, bf16[2048,1152]{1,0:T(8,128)(2,1)}, bf16[1152,2048]{1,0:T(8,128)(2,1)}) custom-call(bf16[2048,1152]{1,0:T(8,128)(2,1)} %bitcast.26, bf16[2048,4608]{1,0:T(8,128)(2,1)} %get-tuple-element.46.hid, bf16[2,4608,1152]{2,1,0:T(8,128)(2,1)} %wd.5), custom_call_target="tpu_custom_call" | custom-call | flops 21743271936 | bytes 29491200 | tf_op jit(solution)/shard_map/down_forward/pallas_call | solution.py:116
  103.6 84.4 %last_layer.1 = (bf16[2048,4608]{1,0:T(8,128)(2,1)}, bf16[2048,4608]{1,0:T(8,128)(2,1)}, bf16[2048,4608]{1,0:T(8,128)(2,1)}) custom-call(bf16[2048,1152]{1,0:T(8,128)(2,1)} %get-tuple-element.48.a, bf16[2048,1152]{1,0:T(8,128)(2,1)} %bitcast.27, bf16[2,1152,4608]{2,1,0:T(8,128)(2,1)} %wg.7, bf16[2,1152,4608]{2,1,0:T(8,128)(2,1)} %wu.7, bf16[2,4608,1152]{2,1,0:T(8,128)(2,1)} %wd.5), custom_call_target="tpu_custom_call" | custom-call | flops 65229815808 | bytes 88473600 | tf_op jit(solution)/shard_map/last_layer/pallas_call | solution.py:153
  187.9 58.4 %gate_up_gradient_1.1.rest_0_ = bf16[16,3,72,2304]{3,2,1,0:T(8,128)(2,1)} custom-call(bf16[1152,2048]{1,0:T(8,128)(2,1)} %get-tuple-element.52.a_t, bf16[2048,4608]{1,0:T(8,128)(2,1)} %get-tuple-element.53.dg0.dg1.dg, bf16[2048,4608]{1,0:T(8,128)(2,1)} %get-tuple-element.53.dg0.dg1.dg, bf16[2048,4608]{1,0:T(8,128)(2,1)} %get-tuple-element.54.du0.du1.du, ...), custom_call_target="tpu_custom_call" | custom-call | flops 43486543872 | bytes 37748736 | tf_op jit(solution)/shard_map/gate_up_gradient_1/pallas_call | solution.py:362
  246.4 34.5 %down_gradient_2.1 = bf16[16,3,72,2304]{3,2,1,0:T(8,128)(2,1)} custom-call(bf16[2048,4608]{1,0:T(8,128)(2,1)} %get-tuple-element.51.hid, bf16[2048,1152]{1,0:T(8,128)(2,1)} %bitcast.28, bf16[16,3,72,2304]{3,2,1,0:T(8,128)(2,1)} %gate_up_gradient_1.1.rest_0_), custom_call_target="tpu_custom_call", output_to_operand_aliasing={{}: (2, {})} | custom-call | flops 21743271936 | bytes 24182784 | tf_op jit(solution)/shard_map/down_gradient_2/pallas_call | solution.py:307
  280.8 0.1 reduce-scatter.7.cloned.1.call-update
  280.9 0.1 reduce-scatter.9.cloned.1.call-start
  281.0 60.7 %states_cotangent.1.dy = bf16[2048,1152]{1,0:T(8,128)(2,1)} custom-call(bf16[2048,1152]{1,0:T(8,128)(2,1)} %get-tuple-element.47.h, bf16[2048,1152]{1,0:T(8,128)(2,1)} %bitcast.29, bf16[2048,4608]{1,0:T(8,128)(2,1)} %get-tuple-element.53.dg0.dg1.dg, bf16[2048,4608]{1,0:T(8,128)(2,1)} %get-tuple-element.54.du0.du1.du, bf16[2,1152,4608]{2,1,0:T(8,128)(2,1)} %wg.7, ...), custom_call_target="tpu_custom_call" | custom-call | flops 43486543872 | bytes 58982400 | tf_op jit(solution)/shard_map/states_cotangent/pallas_call | solution.py:208
  341.7 34.6 %down_gradient_3.1 = bf16[2304,1152]{1,0:T(8,128)(2,1)} custom-call(bf16[2048,4608]{1,0:T(8,128)(2,1)} %get-tuple-element.46.hid, bf16[2048,1152]{1,0:T(8,128)(2,1)} %states_cotangent.1.dy), custom_call_target="tpu_custom_call" | custom-call | flops 21743271936 | bytes 24182784 | tf_op jit(solution)/shard_map/down_gradient_3/pallas_call | solution.py:307
  376.2 0.1 reduce-scatter.9.cloned.1.call-update
  376.3 0.1 all-gather.2.cloned.1.call-start
  376.4 122.9 %first_layer_gradient.1.gu0 = bf16[2,72,2304]{2,1,0:T(8,128)(2,1)} custom-call(bf16[1152,2048]{1,0:T(8,128)(2,1)} %get-tuple-element.45.a_t, bf16[2048,1152]{1,0:T(8,128)(2,1)} %states_cotangent.1.dy, f32[2048,4608]{1,0:T(8,128)} %get-tuple-element.56.g0.g1, f32[2048,4608]{1,0:T(8,128)} %get-tuple-element.56.g0.g1, f32[2048,4608]{1,0:T(8,128)} %get-tuple-element.57.u0.u1, ...), custom_call_target="tpu_custom_call" | custom-call | flops 65229815808 | bytes 75497472 | tf_op jit(solution)/shard_map/first_layer_gradient/pallas_call | solution.py:534
  499.3 0.0 reduce-scatter.7.cloned.1.call-done
  499.3 0.0 reduce-scatter.9.cloned.1.call-done.d0
  499.3 158.8 %updated_and_gathered.1 = (bf16[4,4,2,2,72,5760]{5,4,3,2,1,0:T(8,128)(2,1)}, bf16[144,1152]{1,0:T(8,128)(2,1)}, f32[36,2,4608]{2,1,0:T(2,128)}, f32[36,2,4608]{2...) custom-call(bf16[2,72,2304]{2,1,0:T(8,128)(2,1)} %first_layer_gradie, ...), custom_call_target="tpu_custom_call" | custom-call | flops 1000000000 | bytes 100000000 | tf_op jit(solution)/shard_map/updated_and_gathered/pallas_call | solution.py:796
  658.2 0.1 all-gather.2.cloned.1.call-update
  658.2 33.6 %placed.1 = (bf16[2,1152,4608]{2,1,0:T(8,128)(2,1)}, bf16[2,1152,4608]{2,1,0:T(8,128)(2,1)}, bf16[2,4608,1152]{2,1,0:T(8,128)(2,1)}) custom-call(bf16[4,4,2,2,72,5760]{5,4,3,2,1,0:T(8,128)(2,1)} %get-tuple-element.64.t), custom_call_target="tpu_custom_call" | custom-call | flops 1 | bytes 106168320 | tf_op jit(solution)/shard_map/placed/pallas_call | solution.py:848
  691.8 6.7 copied.1
  698.5 10.3 %all-gather.2.cloned.1.call-done.t = bf16[4608,1152]{1,0:T(8,128)(2,1)} async-done(((bf16[144,1152]{1,0:T(8,128)(2,1)}), bf16[4608,1152]{1,0:T(8,128)(2,1)}) %all-gather.2.cloned.1.call-update) | async-done | bytes 10616848 | tf_op jit(solution)/shard_map/all_gather | solution.py:926
  708.8 8.3 %placed_last.1 = bf16[2,4608,1152]{2,1,0:T(8,128)(2,1)} custom-call(bf16[2,4608,1152]{2,1,0:T(8,128)(2,1)} %get-tuple-element.67.down, bf16[4608,1152]{1,0:T(8,128)(2,1)} %all-gather.2.cloned.1.call-done.t), custom_call_target="tpu_custom_call", output_to_operand_aliasing={{}: (0, {})} | custom-call | flops 1 | bytes 21233664 | tf_op jit(solution)/shard_map/placed_last/pallas_call | solution.py:887
Async XLA Ops:
  7.2 492.1 %reduce-scatter.7.cloned.1.call-start = ((), (), s32[]{:S(2)}) async-start(), calls=%async_computation.3 | async-start | bytes 16920576
  280.9 218.4 %reduce-scatter.9.cloned.1.call-start = ((), (), s32[]{:S(2)}) async-start(), calls=%async_computation.4 | async-start | bytes 5640192
  376.3 332.5 %all-gather.2.cloned.1.call-start = ((), (), s32[]{:S(2)}) async-start(), calls=%async_computation.2 | async-start | bytes 10948608 | tf_op jit(solution)/shard_map/all_gather | solution.py:926
Sparse Core Ops, SparseCore 0:
  281.0 105.8 reduce-scatter.6
  390.3 81.8 reduce-scatter.8
  658.4 50.3 all-gather.1

commit v3 on v2

--- a/solution.py
+++ b/solution.py
@@ -522,10 +522,10 @@
                 made[slot, h, :, PART:] = dot(a_t[...], du[h]).astype(BF16)
             swap(block).start()
 
-        stage(8, last)
-        stage(7, fourth)
-        stage(6, third)
-        stage(4, second)
+        stage(7, last)
+        stage(6, fourth)
+        stage(5, third)
+        stage(3, second)
         stage(2, first)
         stage(0, make)
 
@@ -537,9 +537,9 @@
         16 * tokens * PART * n,
         pair_params(number),
         name="first_layer_gradient",
-        grid=(n + 8,),
+        grid=(n + 7,),
         in_specs=[whole((d, tokens)), whole((tokens, d)), *t_specs, *t_specs, *halves_specs((None, PART, d), 0, n, half, layer, True)],
-        out_specs=pl.BlockSpec((2, rows, PART), lambda j: (0, 0, jnp.maximum(j - 8, 0))),
+        out_specs=pl.BlockSpec((2, rows, PART), lambda j: (0, 0, jnp.maximum(j - 7, 0))),
         out_shape=jax.ShapeDtypeStruct((2, rows, PART * n), BF16),
         scratch_shapes=[
             pltpu.VMEM((2, tokens, PART), BF16),

time: 731 us -> 731 us (level)
  transfers between devices with their start and end apart: 3 -> 3, of which waited for: 1 -> 1; matrix products, arithmetic and copies ran while one was open for 0% -> 0% of each run, Pallas kernels for 36% -> 35%
where the time goes in v3:
time: 731 us; the launch traced here: 725 us
  Pallas kernels  699 us (96%)
  between operations  14.4 us (2%)
  waiting for transfers between devices  10.9 us (1%)
    pallas_call x1, Pallas kernels, updated_and_gathered(): call(body, 1000000000.0, 100000000.0, pair_params(number), name='updated_...  161 us
    pallas_call x1, Pallas kernels, first_layer_gradient(): call(body, 12 * tokens * d * PART * n, 16 * tokens * PART * n, pair_param...  121 us
    pallas_call x1, Pallas kernels, last_layer(): call(body, 6 * tokens * d * ff, 6 * tokens * ff + 6 * d * ff, name='last_...  84.4 us
    pallas_call x2, Pallas kernels, down_gradient(): call(body, 2 * tokens * d * ff, 2 * tokens * ff + d * ff, pair_params(num...  69.1 us
    pallas_call x1, Pallas kernels, hidden_forward(): call(body, 4 * tokens * d * ff, 10 * tokens * ff + 4 * d * ff, name='hidd...  61.2 us
    pallas_call x1, Pallas kernels, states_cotangent(): call(body, 4 * tokens * d * ff, 4 * tokens * ff + 4 * d * ff, name='state...  60.7 us
    pallas_call x1, Pallas kernels, gate_up_gradient(): call(body, 8 * tokens * d * PART * n, 8 * tokens * PART * n, pair_params(...  58.4 us
    pallas_call x1, Pallas kernels, down_forward(): call(body, 2 * tokens * d * ff, 2 * tokens * ff + 2 * d * ff, name='down_...  35.1 us
  transfers between devices with their start and end apart: 3, of which 1 were waited for; matrix products, arithmetic and copies ran while one was open for 0% of the time, Pallas kernels for 35%

profile of v3, /device:TPU:97, one launch (start us, length us, event | category | flops | bytes accessed | tf_op | source)
XLA Modules:
  0.0 724.7 jit_solution(14337435249764739262)
XLA Ops:
  7.2 0.1 reduce-scatter.7.cloned.1.call-start
  7.3 61.2 %hidden_forward.1 = (f32[2048,4608]{1,0:T(8,128)}, f32[2048,4608]{1,0:T(8,128)}, bf16[2048,4608]{1,0:T(8,128)(2,1)}, bf16[1152,2048]{1,0:T(8,128)(2,1)}) custom-call(bf16[2048,1152]{1,0:T(8,128)(2,1)} %bitcast.25, bf16[2,1152,4608]{2,1,0:T(8,128)(2,1)} %wg.7, bf16[2,1152,4608]{2,1,0:T(8,128)(2,1)} %wu.7), custom_call_target="tpu_custom_call" | custom-call | flops 43486543872 | bytes 115605504 | tf_op jit(solution)/shard_map/hidden_forward/pallas_call | solution.py:88
  68.5 35.1 %down_forward.1 = (bf16[2048,1152]{1,0:T(8,128)(2,1)}, bf16[2048,1152]{1,0:T(8,128)(2,1)}, bf16[1152,2048]{1,0:T(8,128)(2,1)}) custom-call(bf16[2048,1152]{1,0:T(8,128)(2,1)} %bitcast.26, bf16[2048,4608]{1,0:T(8,128)(2,1)} %get-tuple-element.46.hid, bf16[2,4608,1152]{2,1,0:T(8,128)(2,1)} %wd.5), custom_call_target="tpu_custom_call" | custom-call | flops 21743271936 | bytes 29491200 | tf_op jit(solution)/shard_map/down_forward/pallas_call | solution.py:116
  103.6 84.4 %last_layer.1 = (bf16[2048,4608]{1,0:T(8,128)(2,1)}, bf16[2048,4608]{1,0:T(8,128)(2,1)}, bf16[2048,4608]{1,0:T(8,128)(2,1)}) custom-call(bf16[2048,1152]{1,0:T(8,128)(2,1)} %get-tuple-element.48.a, bf16[2048,1152]{1,0:T(8,128)(2,1)} %bitcast.27, bf16[2,1152,4608]{2,1,0:T(8,128)(2,1)} %wg.7, bf16[2,1152,4608]{2,1,0:T(8,128)(2,1)} %wu.7, bf16[2,4608,1152]{2,1,0:T(8,128)(2,1)} %wd.5), custom_call_target="tpu_custom_call" | custom-call | flops 65229815808 | bytes 88473600 | tf_op jit(solution)/shard_map/last_layer/pallas_call | solution.py:153
  187.9 58.4 %gate_up_gradient_1.1.rest_0_ = bf16[16,3,72,2304]{3,2,1,0:T(8,128)(2,1)} custom-call(bf16[1152,2048]{1,0:T(8,128)(2,1)} %get-tuple-element.52.a_t, bf16[2048,4608]{1,0:T(8,128)(2,1)} %get-tuple-element.53.dg0.dg1.dg, bf16[2048,4608]{1,0:T(8,128)(2,1)} %get-tuple-element.53.dg0.dg1.dg, bf16[2048,4608]{1,0:T(8,128)(2,1)} %get-tuple-element.54.du0.du1.du, ...), custom_call_target="tpu_custom_call" | custom-call | flops 43486543872 | bytes 37748736 | tf_op jit(solution)/shard_map/gate_up_gradient_1/pallas_call | solution.py:362
  246.4 34.5 %down_gradient_2.1 = bf16[16,3,72,2304]{3,2,1,0:T(8,128)(2,1)} custom-call(bf16[2048,4608]{1,0:T(8,128)(2,1)} %get-tuple-element.51.hid, bf16[2048,1152]{1,0:T(8,128)(2,1)} %bitcast.28, bf16[16,3,72,2304]{3,2,1,0:T(8,128)(2,1)} %gate_up_gradient_1.1.rest_0_), custom_call_target="tpu_custom_call", output_to_operand_aliasing={{}: (2, {})} | custom-call | flops 21743271936 | bytes 24182784 | tf_op jit(solution)/shard_map/down_gradient_2/pallas_call | solution.py:307
  280.8 0.1 reduce-scatter.7.cloned.1.call-update
  280.9 0.1 reduce-scatter.9.cloned.1.call-start
  281.0 60.7 %states_cotangent.1.dy = bf16[2048,1152]{1,0:T(8,128)(2,1)} custom-call(bf16[2048,1152]{1,0:T(8,128)(2,1)} %get-tuple-element.47.h, bf16[2048,1152]{1,0:T(8,128)(2,1)} %bitcast.29, bf16[2048,4608]{1,0:T(8,128)(2,1)} %get-tuple-element.53.dg0.dg1.dg, bf16[2048,4608]{1,0:T(8,128)(2,1)} %get-tuple-element.54.du0.du1.du, bf16[2,1152,4608]{2,1,0:T(8,128)(2,1)} %wg.7, ...), custom_call_target="tpu_custom_call" | custom-call | flops 43486543872 | bytes 58982400 | tf_op jit(solution)/shard_map/states_cotangent/pallas_call | solution.py:208
  341.7 34.6 %down_gradient_3.1 = bf16[2304,1152]{1,0:T(8,128)(2,1)} custom-call(bf16[2048,4608]{1,0:T(8,128)(2,1)} %get-tuple-element.46.hid, bf16[2048,1152]{1,0:T(8,128)(2,1)} %states_cotangent.1.dy), custom_call_target="tpu_custom_call" | custom-call | flops 21743271936 | bytes 24182784 | tf_op jit(solution)/shard_map/down_gradient_3/pallas_call | solution.py:307
  376.2 0.1 reduce-scatter.9.cloned.1.call-update
  376.3 0.1 all-gather.2.cloned.1.call-start
  376.4 120.8 %first_layer_gradient.1.gu0 = bf16[2,72,2304]{2,1,0:T(8,128)(2,1)} custom-call(bf16[1152,2048]{1,0:T(8,128)(2,1)} %get-tuple-element.45.a_t, bf16[2048,1152]{1,0:T(8,128)(2,1)} %states_cotangent.1.dy, f32[2048,4608]{1,0:T(8,128)} %get-tuple-element.56.g0.g1, f32[2048,4608]{1,0:T(8,128)} %get-tuple-element.56.g0.g1, f32[2048,4608]{1,0:T(8,128)} %get-tuple-element.57.u0.u1, ...), custom_call_target="tpu_custom_call" | custom-call | flops 65229815808 | bytes 75497472 | tf_op jit(solution)/shard_map/first_layer_gradient/pallas_call | solution.py:534
  497.1 0.0 reduce-scatter.7.cloned.1.call-done
  497.2 0.0 reduce-scatter.9.cloned.1.call-done.d0
  497.2 161.1 %updated_and_gathered.1 = (bf16[4,4,2,2,72,5760]{5,4,3,2,1,0:T(8,128)(2,1)}, bf16[144,1152]{1,0:T(8,128)(2,1)}, f32[36,2,4608]{2,1,0:T(2,128)}, f32[36,2,4608]{2...) custom-call(bf16[2,72,2304]{2,1,0:T(8,128)(2,1)} %first_layer_gradie, ...), custom_call_target="tpu_custom_call" | custom-call | flops 1000000000 | bytes 100000000 | tf_op jit(solution)/shard_map/updated_and_gathered/pallas_call | solution.py:796
  658.3 0.1 all-gather.2.cloned.1.call-update
  658.3 33.6 %placed.1 = (bf16[2,1152,4608]{2,1,0:T(8,128)(2,1)}, bf16[2,1152,4608]{2,1,0:T(8,128)(2,1)}, bf16[2,4608,1152]{2,1,0:T(8,128)(2,1)}) custom-call(bf16[4,4,2,2,72,5760]{5,4,3,2,1,0:T(8,128)(2,1)} %get-tuple-element.64.t), custom_call_target="tpu_custom_call" | custom-call | flops 1 | bytes 106168320 | tf_op jit(solution)/shard_map/placed/pallas_call | solution.py:848
  691.9 6.7 copied.1
  698.6 10.7 %all-gather.2.cloned.1.call-done.t = bf16[4608,1152]{1,0:T(8,128)(2,1)} async-done(((bf16[144,1152]{1,0:T(8,128)(2,1)}), bf16[4608,1152]{1,0:T(8,128)(2,1)}) %all-gather.2.cloned.1.call-update) | async-done | bytes 10616848 | tf_op jit(solution)/shard_map/all_gather | solution.py:926
  709.3 8.3 %placed_last.1 = bf16[2,4608,1152]{2,1,0:T(8,128)(2,1)} custom-call(bf16[2,4608,1152]{2,1,0:T(8,128)(2,1)} %get-tuple-element.67.down, bf16[4608,1152]{1,0:T(8,128)(2,1)} %all-gather.2.cloned.1.call-done.t), custom_call_target="tpu_custom_call", output_to_operand_aliasing={{}: (0, {})} | custom-call | flops 1 | bytes 21233664 | tf_op jit(solution)/shard_map/placed_last/pallas_call | solution.py:887
Async XLA Ops:
  7.2 490.0 %reduce-scatter.7.cloned.1.call-start = ((), (), s32[]{:S(2)}) async-start(), calls=%async_computation.3 | async-start | bytes 16920576
  280.9 216.3 %reduce-scatter.9.cloned.1.call-start = ((), (), s32[]{:S(2)}) async-start(), calls=%async_computation.4 | async-start | bytes 5640192
  376.3 333.0 %all-gather.2.cloned.1.call-start = ((), (), s32[]{:S(2)}) async-start(), calls=%async_computation.2 | async-start | bytes 10948608 | tf_op jit(solution)/shard_map/all_gather | solution.py:926
Sparse Core Ops, SparseCore 0:
  281.0 105.8 reduce-scatter.6
  390.3 81.7 reduce-scatter.8
  658.5 50.8 all-gather.1
